TPU v7x, 32 devices: a whole 2x2x4 slice. The times are simulated.
32 devices in a mesh: gz: 4 (over y, core), gy: 2 (over x), gx: 4 (over z).
Axes of the slice: x: 2, y: 2, z: 4, core: 2. Of those that a mesh axis runs over, the one named last changes fastest.
Arguments:
- positions: float32 [3, 4, 4, 32, 128], P(None, 'gx', 'gy', 'gz'), may hold values from 0 to 1
- counts: int32 [4, 4, 32], P('gx', 'gy', 'gz'), may hold values from 104 to 128
Outputs:
- energy: float32 [4, 4, 32, 128], P('gx', 'gy', 'gz')
- forces: float32 [3, 4, 4, 32, 128], P(None, 'gx', 'gy', 'gz')
Inputs may be any that keep to these rules, and one draw needn't show every extreme that they name: `counts`: slot k of a cell holds an atom exactly when k < its count; positions of other slots are not used.
All inputs are finite; a program needn't handle non-finite values.
Results may differ from a plain program's by a relative error of at most 0.0003.
Values sent between devices are 32-bit elements; how exact they have to be, the bound alone decides.
A program may use at most 64 MiB of HBM per device.

v0:
```python
import jax
import jax.numpy as jnp
from jax import lax
from jax.sharding import PartitionSpec as P

SENTINEL = 4.0
PAIR_SCALE = 0.02
EMBED_SCALE = 0.2
CUTOFF_SQUARED = 0.25
FORCE_SCALE = 8.0
neighbour_offsets = [
    (step_x, step_y, step_z)
    for step_x in (-1, 0, 1)
    for step_y in (-1, 0, 1)
    for step_z in (-1, 0, 1)
]


def with_halo(block, sides, width):
    for axis, dim in sides:
        count = lax.axis_size(axis)
        forward = [(i, i + 1) for i in range(count - 1)]
        forward.append((count - 1, 0))
        backward = [(target, source) for source, target in forward]
        low = lax.ppermute(
            lax.slice_in_dim(block, block.shape[dim] - width, None, axis=dim), axis, forward
        )
        high = lax.ppermute(lax.slice_in_dim(block, 0, width, axis=dim), axis, backward)
        block = jnp.concatenate([low, block, high], axis=dim)
    return block


def pair_geometry(own_cells, far_cells, offset):
    deltas = []
    for component in range(3):
        deltas.append(
            far_cells[component][..., None, :]
            - own_cells[component][..., :, None]
            + offset[component]
        )
    return deltas


def density_terms(own_cells, far_cells, offset, itself):
    deltas = pair_geometry(own_cells, far_cells, offset)
    squared = deltas[0] * deltas[0] + deltas[1] * deltas[1] + deltas[2] * deltas[2]
    weight = jnp.maximum(1.0 - squared / CUTOFF_SQUARED, 0.0)
    square = weight * weight
    if itself:
        slot_count = own_cells.shape[-1]
        square = jnp.where(jnp.eye(slot_count, dtype=bool), 0.0, square)
    return (jnp.sum(square, -1), jnp.sum(PAIR_SCALE * (square * square - 2.0 * square), -1))


def force_terms(own_cells, far_cells, own_fp, far_fp, offset):
    deltas = pair_geometry(own_cells, far_cells, offset)
    squared = deltas[0] * deltas[0] + deltas[1] * deltas[1] + deltas[2] * deltas[2]
    weight = jnp.maximum(1.0 - squared / CUTOFF_SQUARED, 0.0)
    factor = (own_fp[..., :, None] + far_fp[..., None, :]) * (
        -2.0 * weight
    ) + 4.0 * PAIR_SCALE * weight * (1.0 - weight * weight)
    return jnp.stack([FORCE_SCALE * jnp.sum(factor * delta, -1) for delta in deltas])


def settle(stacked, layers):
    lower_rim = stacked[:, :, :, 0:1]
    upper_rim = stacked[:, :, :, layers + 1 : layers + 2]
    both_rims = jnp.concatenate([lower_rim, upper_rim], axis=3)
    returned = with_halo(both_rims, (("gz", 3),), 1)
    interior = stacked[:, :, :, 1 : layers + 1]
    interior = interior.at[:, :, :, 0].add(returned[:, :, :, 0])
    interior = interior.at[:, :, :, layers - 1].add(returned[:, :, :, 3])
    return interior


def per_device(positions, counts):
    slot_count = positions.shape[-1]
    across = positions.shape[1]
    breadth = positions.shape[2]
    layers = positions.shape[3]
    occupied = jnp.arange(slot_count, dtype=jnp.int32) < counts[..., None]
    seated = jnp.where(occupied[None], positions, SENTINEL)
    tower_block = with_halo(seated, (("gz", 3),), 1)
    plate_block = with_halo(seated, (("gy", 2), ("gx", 1)), 1)
    totals = jnp.zeros((2, across, breadth, layers + 2, slot_count), jnp.float32)
    for step_x, step_y, step_z in neighbour_offsets:
        own_cells = tower_block[:, :, :, 1 + step_z : 1 + step_z + layers]
        far_cells = plate_block[
            :, 1 + step_x : 1 + step_x + across, 1 + step_y : 1 + step_y + breadth
        ]
        itself = step_x == 0 and step_y == 0 and (step_z == 0)
        rho_part, pair_part = density_terms(own_cells, far_cells, (step_x, step_y, -step_z), itself)
        totals = totals.at[:, :, :, 1 + step_z : 1 + step_z + layers].add(
            jnp.stack([rho_part, pair_part])
        )
    density = settle(totals, layers)
    rho_sum = density[0]
    pair_sum = density[1]
    fprime = -0.5 * EMBED_SCALE * lax.rsqrt(rho_sum + 1.0)
    tower_fp = with_halo(fprime, (("gz", 2),), 1)
    plate_fp = with_halo(fprime, (("gy", 1), ("gx", 0)), 1)
    pushes = jnp.zeros((3, across, breadth, layers + 2, slot_count), jnp.float32)
    for step_x, step_y, step_z in neighbour_offsets:
        own_cells = tower_block[:, :, :, 1 + step_z : 1 + step_z + layers]
        far_cells = plate_block[
            :, 1 + step_x : 1 + step_x + across, 1 + step_y : 1 + step_y + breadth
        ]
        own_fp = tower_fp[:, :, 1 + step_z : 1 + step_z + layers]
        far_fp = plate_fp[1 + step_x : 1 + step_x + across, 1 + step_y : 1 + step_y + breadth]
        pushes = pushes.at[:, :, :, 1 + step_z : 1 + step_z + layers].add(
            force_terms(own_cells, far_cells, own_fp, far_fp, (step_x, step_y, -step_z))
        )
    forces = settle(pushes, layers)
    energy = jnp.where(occupied, -EMBED_SCALE * jnp.sqrt(rho_sum + 1.0) + 0.5 * pair_sum, 0.0)
    forces = jnp.where(occupied[None], forces, 0.0)
    return (energy, forces)


def solution(mesh):
    placed = (P(None, "gx", "gy", "gz", None), P("gx", "gy", "gz"))
    return jax.shard_map(
        per_device,
        mesh=mesh,
        in_specs=placed,
        out_specs=(P("gx", "gy", "gz", None), P(None, "gx", "gy", "gz", None)),
        check_vma=False,
    )
```

profile of v0, /device:TPU:0, one launch (start us, length us, event | category | flops | bytes accessed | tf_op | source)
XLA Modules:
  0.0 118.8 jit_solution(18105359406716745990)
XLA Ops:
  0.6 0.7 copy-done
  1.4 0.7 broadcast_select_fusion.1
  2.1 3.0 %collective-permute-start.1 = (f32[3,1,1,8,128]{4,3,2,1,0:T(8,128)S(1)}, f32[3,1,1,8,128]{4,3,2,1,0:T(8,128)S(1)}, u32[]{:S(2)}, u32[]{:S(2)}) collective-permute-start(f32[3,1,1,8,128]{4,3,2,1,0:T(8,128)S(1)} %get-tuple-element.980), channel_id=1, source_target_pairs={{4,0},{0,4},{5,1},{1,5},{6,2},{2,6},{7,3},{3,7},{12,8},{8,12},{13,... | collective-permute-start | bytes 36872 | tf_op jit(solution)/shard_map/ppermute | solution.py:28
  5.2 0.9 collective-permute-start.4
  6.1 3.0 %collective-permute-done.3 = f32[3,1,2,1,128]{4,3,2,1,0:T(1,128)S(1)} collective-permute-done((f32[3,1,2,1,128]{4,3,2,1,0:T(1,128)S(1)}, f32[3,1,2,1,128]{4,3,2,1,0:T(1,128)S(1)}, u32[]{:S(2)}, u32[]{:S(2)}) %collective-permute-start.3) | collective-permute-done | bytes 3104 | tf_op jit(solution)/shard_map/ppermute | solution.py:25
  9.1 1.6 %collective-permute-start.2 = (f32[3,1,4,8,128]{4,3,2,1,0:T(8,128)S(1)}, f32[3,1,4,8,128]{4,3,2,1,0:T(8,128)S(1)}, u32[]{:S(2)}, u32[]{:S(2)}) collective-permute-start(f32[3,1,4,8,128]{4,3,2,1,0:T(8,128)S(1)} %pad_maximum_fusion), channel_id=1, source_target_pairs={{0,1},{1,2},{2,3},{3,0},{4,5},{5,6},{6,7},{7,4},{8,9},{9,10},{10,1... | collective-permute-start | bytes 147464 | tf_op jit(solution)/shard_map/ppermute | solution.py:25
  10.7 2.2 %collective-permute-start.5 = (f32[3,1,4,8,128]{4,3,2,1,0:T(8,128)S(1)}, f32[3,1,4,8,128]{4,3,2,1,0:T(8,128)S(1)}, u32[]{:S(2)}, u32[]{:S(2)}) collective-permute-start(f32[3,1,4,8,128]{4,3,2,1,0:T(8,128)S(1)} %pad_maximum_fusion), channel_id=1, source_target_pairs={{1,0},{2,1},{3,2},{0,3},{5,4},{6,5},{7,6},{4,7},{9,8},{10,9},{11,1... | collective-permute-start | bytes 147464 | tf_op jit(solution)/shard_map/ppermute | solution.py:28
  13.0 2.2 %collective-permute-done.2 = f32[3,1,4,8,128]{4,3,2,1,0:T(8,128)S(1)} collective-permute-done((f32[3,1,4,8,128]{4,3,2,1,0:T(8,128)S(1)}, f32[3,1,4,8,128]{4,3,2,1,0:T(8,128)S(1)}, u32[]{:S(2)}, u32[]{:S(2)}) %collective-permute-start.2) | collective-permute-done | bytes 49184 | tf_op jit(solution)/shard_map/ppermute | solution.py:25
  15.2 6.8 %multiply_reduce_fusion.84 = (f32[2,8,128]{2,1,0:T(8,128)S(1)}, f32[2,8,128]{2,1,0:T(8,128)S(1)}, f32[2,8,128]{2,1,0:T(8,128)S(1)}, f32[2,8,128]{2,1,0:T(8,128)S...) fusion(f32[2,8,128]{2,1,0:T(8,128)S(1)} %get-tuple-element.972,, ...), kind=kLoop, calls=%fused_computation.315 | loop fusion | flops 31694848 | bytes 221184 | tf_op jit(solution)/shard_map/reduce_sum | solution.py:52
  22.0 0.1 scatter-add.195
  22.2 0.1 scatter-add.196
  22.4 11.6 %multiply_reduce_fusion.55 = (f32[2,8,128]{2,1,0:T(8,128)S(1)}, f32[2,8,128]{2,1,0:T(8,128)S(1)}, f32[2,8,128]{2,1,0:T(8,128)S(1)}, f32[2,8,128]{2,1,0:T(8,128)S...) fusion(f32[2,8,128]{2,1,0:T(8,128)S(1)} %get-tuple-element.972,, ...), kind=kLoop, calls=%fused_computation.254 | loop fusion | flops 62078976 | bytes 360448 | tf_op jit(solution)/shard_map/reduce_sum | solution.py:52
  34.0 0.1 scatter-add.200
  34.1 0.1 scatter-add.201
  34.2 9.1 %multiply_reduce_fusion.67 = (f32[2,8,128]{2,1,0:T(8,128)S(1)}, f32[2,8,128]{2,1,0:T(8,128)S(1)}, f32[2,8,128]{2,1,0:T(8,128)S(1)}, f32[2,8,128]{2,1,0:T(8,128)S...) fusion(f32[2,8,128]{2,1,0:T(8,128)S(1)} %get-tuple-element.972,, ...), kind=kLoop, calls=%fused_computation.281 | loop fusion | flops 47935488 | bytes 294912 | tf_op jit(solution)/shard_map/reduce_sum | solution.py:52
  43.4 0.1 scatter-add.205
  43.5 0.1 scatter-add.206
  43.7 0.1 scatter-add.210
  43.9 0.1 scatter-add.211
  44.0 0.1 scatter-add.215
  44.2 0.1 scatter-add.216
  44.3 0.1 scatter-add.220
  44.5 0.1 scatter-add.221
  44.8 0.1 scatter-add.226
  45.3 0.1 scatter-add.235
  45.7 2.9 %collective-permute-done.6 = f32[2,1,2,1,128]{4,3,2,1,0:T(1,128)S(1)} collective-permute-done((f32[2,1,2,1,128]{4,3,2,1,0:T(1,128)S(1)}, f32[2,1,2,1,128]{4,3,2,1,0:T(1,128)S(1)}, u32[]{:S(2)}, u32[]{:S(2)}) %collective-permute-start.6) | collective-permute-done | bytes 2080 | tf_op jit(solution)/shard_map/ppermute | solution.py:25
  48.6 1.3 %collective-permute-done.7 = f32[2,1,2,1,128]{4,3,2,1,0:T(1,128)S(1)} collective-permute-done((f32[2,1,2,1,128]{4,3,2,1,0:T(1,128)S(1)}, f32[2,1,2,1,128]{4,3,2,1,0:T(1,128)S(1)}, u32[]{:S(2)}, u32[]{:S(2)}) %collective-permute-start.7) | collective-permute-done | bytes 2080 | tf_op jit(solution)/shard_map/ppermute | solution.py:28
  49.9 1.6 %collective-permute-start.10 = (f32[1,1,8,128]{3,2,1,0:T(8,128)S(1)}, f32[1,1,8,128]{3,2,1,0:T(8,128)S(1)}, u32[]{:S(2)}, u32[]{:S(2)}) collective-permute-start(f32[1,1,8,128]{3,2,1,0:T(8,128)S(1)} %get-tuple-element.997), channel_id=1, source_target_pairs={{4,0},{0,4},{5,1},{1,5},{6,2},{2,6},{7,3},{3,7},{12,8},{8,12},{13,... | collective-permute-start | bytes 12296 | tf_op jit(solution)/shard_map/ppermute | solution.py:28
  51.5 0.5 collective-permute-start.9
  52.0 0.6 collective-permute-start.8
  52.6 1.1 collective-permute-start.12
  53.7 1.3 %collective-permute-done.9 = f32[1,1,8,128]{3,2,1,0:T(8,128)S(1)} collective-permute-done((f32[1,1,8,128]{3,2,1,0:T(8,128)S(1)}, f32[1,1,8,128]{3,2,1,0:T(8,128)S(1)}, u32[]{:S(2)}, u32[]{:S(2)}) %collective-permute-start.9) | collective-permute-done | bytes 4128 | tf_op jit(solution)/shard_map/ppermute | solution.py:25
  55.1 3.8 %collective-permute-start.13 = (f32[1,4,8,128]{3,2,1,0:T(8,128)S(1)}, f32[1,4,8,128]{3,2,1,0:T(8,128)S(1)}, u32[]{:S(2)}, u32[]{:S(2)}) collective-permute-start(f32[1,4,8,128]{3,2,1,0:T(8,128)S(1)} %pad_maximum_fusion.1), channel_id=1, source_target_pairs={{1,0},{2,1},{3,2},{0,3},{5,4},{6,5},{7,6},{4,7},{9,8},{10,9},{11,1... | collective-permute-start | bytes 49160 | tf_op jit(solution)/shard_map/ppermute | solution.py:28
  58.9 1.7 %collective-permute-done.11 = f32[1,4,8,128]{3,2,1,0:T(8,128)S(1)} collective-permute-done((f32[1,4,8,128]{3,2,1,0:T(8,128)S(1)}, f32[1,4,8,128]{3,2,1,0:T(8,128)S(1)}, u32[]{:S(2)}, u32[]{:S(2)}) %collective-permute-start.11) | collective-permute-done | bytes 16416 | tf_op jit(solution)/shard_map/ppermute | solution.py:25
  60.6 5.9 %multiply_reduce_fusion.43 = (f32[2,8,128]{2,1,0:T(8,128)S(1)}, f32[2,8,128]{2,1,0:T(8,128)S(1)}, f32[2,8,128]{2,1,0:T(8,128)S(1)}, f32[2,8,128]{2,1,0:T(8,128)S...) fusion(f32[2,8,128]{2,1,0:T(8,128)S(1)} %get-tuple-element.942,, ...), kind=kLoop, calls=%fused_computation.237 | loop fusion | flops 21215232 | bytes 204800 | tf_op jit(solution)/shard_map/reduce_sum | solution.py:62
  66.5 5.8 %multiply_reduce_fusion.40 = (f32[2,8,128]{2,1,0:T(8,128)S(1)}, f32[2,8,128]{2,1,0:T(8,128)S(1)}, f32[2,8,128]{2,1,0:T(8,128)S(1)}, f32[2,8,128]{2,1,0:T(8,128)S...) fusion(f32[2,8,128]{2,1,0:T(8,128)S(1)} %get-tuple-element.937,, ...), kind=kLoop, calls=%fused_computation.232 | loop fusion | flops 21477376 | bytes 204800 | tf_op jit(solution)/shard_map/reduce_sum | solution.py:62
  72.4 2.4 %multiply_reduce_fusion.53 = (f32[2,8,128]{2,1,0:T(8,128)S(1)}, f32[2,8,128]{2,1,0:T(8,128)S(1)}, f32[2,8,128]{2,1,0:T(8,128)S(1)}) fusion(f32[2,8,128]{2,1,0:T(8,128)S(1)} %get-tuple-element.963, f32[2,8,128]{2,1,0:T(8,128)S(1)} %get-tuple-element.945, f32[2,8,128]{2,1,0:T(8,128)S(1)} %get-tuple-element.964, f32[2,8,128]{2,1,0:T(8,128)S(1)} %get-tuple-element.943, ...), kind=kLoop, calls=%fused_computation.251 | loop fusion | flops 7333888 | bytes 90112 | tf_op jit(solution)/shard_map/reduce_sum | solution.py:62
  74.8 7.6 %multiply_reduce_fusion.15 = (f32[2,8,128]{2,1,0:T(8,128)S(1)}, f32[2,8,128]{2,1,0:T(8,128)S(1)}, f32[2,8,128]{2,1,0:T(8,128)S(1)}, f32[2,8,128]{2,1,0:T(8,128)S...) fusion(f32[2,8,128]{2,1,0:T(8,128)S(1)} %get-tuple-element.946,, ...), kind=kLoop, calls=%fused_computation.193 | loop fusion | flops 28811264 | bytes 229376 | tf_op jit(solution)/shard_map/reduce_sum | solution.py:62
  82.4 5.1 %multiply_reduce_fusion.12 = (f32[2,8,128]{2,1,0:T(8,128)S(1)}, f32[2,8,128]{2,1,0:T(8,128)S(1)}, f32[2,8,128]{2,1,0:T(8,128)S(1)}, f32[2,8,128]{2,1,0:T(8,128)S...) fusion(f32[2,8,128]{2,1,0:T(8,128)S(1)} %get-tuple-element.952,, ...), kind=kLoop, calls=%fused_computation.189 | loop fusion | flops 21477376 | bytes 204800 | tf_op jit(solution)/shard_map/reduce_sum | solution.py:62
  87.5 7.4 %multiply_reduce_fusion.9 = (f32[2,8,128]{2,1,0:T(8,128)S(1)}, f32[2,8,128]{2,1,0:T(8,128)S(1)}, f32[2,8,128]{2,1,0:T(8,128)S(1)}, f32[2,8,128]{2,1,0:T(8,128)S(...) fusion(f32[2,8,128]{2,1,0:T(8,128)S(1)} %get-tuple-element.952,, ...), kind=kLoop, calls=%fused_computation.184 | loop fusion | flops 27762688 | bytes 229376 | tf_op jit(solution)/shard_map/reduce_sum | solution.py:62
  95.0 5.2 %multiply_reduce_fusion.7 = (f32[2,8,128]{2,1,0:T(8,128)S(1)}, f32[2,8,128]{2,1,0:T(8,128)S(1)}, f32[2,8,128]{2,1,0:T(8,128)S(1)}, f32[2,8,128]{2,1,0:T(8,128)S(...) fusion(f32[2,8,128]{2,1,0:T(8,128)S(1)} %get-tuple-element.949,, ...), kind=kLoop, calls=%fused_computation.181 | loop fusion | flops 21215232 | bytes 204800 | tf_op jit(solution)/shard_map/reduce_sum | solution.py:62
  100.2 9.6 %multiply_reduce_fusion.2 = (f32[2,8,128]{2,1,0:T(8,128)S(1)}, f32[2,8,128]{2,1,0:T(8,128)S(1)}, f32[2,8,128]{2,1,0:T(8,128)S(1)}, f32[2,8,128]{2,1,0:T(8,128)S(...) fusion(f32[2,8,128]{2,1,0:T(8,128)S(1)} %get-tuple-element.949,, ...), kind=kLoop, calls=%fused_computation.174 | loop fusion | flops 41644032 | bytes 278528 | tf_op jit(solution)/shard_map/reduce_sum | solution.py:62
  109.9 0.2 scatter-add.244
  110.1 0.2 scatter-add.245
  110.3 0.2 scatter-add.249
  110.5 0.2 scatter-add.250
  110.8 0.2 scatter-add.254
  111.0 0.2 scatter-add.255
  111.2 0.2 scatter-add.259
  111.4 0.2 scatter-add.260
  111.7 0.2 scatter-add.264
  111.9 0.2 scatter-add.265
  112.1 0.2 scatter-add.269
  112.3 0.2 scatter-add.270
  112.6 0.2 scatter-add.274
  112.8 0.2 scatter-add.275
  113.0 0.2 scatter-add.279
  113.2 0.2 scatter-add.280
  113.5 0.2 scatter-add.284
  113.8 0.2 scatter-add.285
  113.9 2.8 %collective-permute-done.14 = f32[3,1,2,1,128]{4,3,2,1,0:T(1,128)S(1)} collective-permute-done((f32[3,1,2,1,128]{4,3,2,1,0:T(1,128)S(1)}, f32[3,1,2,1,128]{4,3,2,1,0:T(1,128)S(1)}, u32[]{:S(2)}, u32[]{:S(2)}) %collective-permute-start.14) | collective-permute-done | bytes 3104 | tf_op jit(solution)/shard_map/ppermute | solution.py:25
  116.8 0.7 fusion.140
  117.6 0.6 collective-permute-done.15
  118.2 0.6 broadcast_select_fusion
  (145 shorter events, 1.8 us)
Async XLA Ops:
  0.6 0.7 copy-start
  2.1 6.9 %collective-permute-start.1 = (f32[3,1,1,8,128]{4,3,2,1,0:T(8,128)S(1)}, f32[3,1,1,8,128]{4,3,2,1,0:T(8,128)S(1)}, u32[]{:S(2)}, u32[]{:S(2)}) collective-permute-start(f32[3,1,1,8,128]{4,3,2,1,0:T(8,128)S(1)} %get-tuple-element.980), channel_id=1, source_target_pairs={{4,0},{0,4},{5,1},{1,5},{6,2},{2,6},{7,3},{3,7},{12,8},{8,12},{13,... | collective-permute-start | bytes 36872 | tf_op jit(solution)/shard_map/ppermute | solution.py:28
  5.1 4.0 %collective-permute-start = (f32[3,1,1,8,128]{4,3,2,1,0:T(8,128)S(1)}, f32[3,1,1,8,128]{4,3,2,1,0:T(8,128)S(1)}, u32[]{:S(2)}, u32[]{:S(2)}) collective-permute-start(f32[3,1,1,8,128]{4,3,2,1,0:T(8,128)S(1)} %get-tuple-element.981), channel_id=1, source_target_pairs={{0,4},{4,0},{1,5},{5,1},{2,6},{6,2},{3,7},{7,3},{8,12},{12,8},{9,1... | collective-permute-start | bytes 36872 | tf_op jit(solution)/shard_map/ppermute | solution.py:25
  5.2 7.8 %collective-permute-start.4 = (f32[3,1,2,1,128]{4,3,2,1,0:T(1,128)S(1)}, f32[3,1,2,1,128]{4,3,2,1,0:T(1,128)S(1)}, u32[]{:S(2)}, u32[]{:S(2)}) collective-permute-start(f32[3,1,2,1,128]{4,3,2,1,0:T(1,128)S(1)} %get-tuple-element.979), channel_id=1, source_target_pairs={{8,0},{16,8},{24,16},{0,24},{9,1},{17,9},{25,17},{1,25},{10,2},{18... | collective-permute-start | bytes 9224 | tf_op jit(solution)/shard_map/ppermute | solution.py:28
  6.0 3.0 %collective-permute-start.3 = (f32[3,1,2,1,128]{4,3,2,1,0:T(1,128)S(1)}, f32[3,1,2,1,128]{4,3,2,1,0:T(1,128)S(1)}, u32[]{:S(2)}, u32[]{:S(2)}) collective-permute-start(f32[3,1,2,1,128]{4,3,2,1,0:T(1,128)S(1)} %get-tuple-element.978), channel_id=1, source_target_pairs={{0,8},{8,16},{16,24},{24,0},{1,9},{9,17},{17,25},{25,1},{2,10},{10... | collective-permute-start | bytes 9224 | tf_op jit(solution)/shard_map/ppermute | solution.py:25
  9.1 6.1 %collective-permute-start.2 = (f32[3,1,4,8,128]{4,3,2,1,0:T(8,128)S(1)}, f32[3,1,4,8,128]{4,3,2,1,0:T(8,128)S(1)}, u32[]{:S(2)}, u32[]{:S(2)}) collective-permute-start(f32[3,1,4,8,128]{4,3,2,1,0:T(8,128)S(1)} %pad_maximum_fusion), channel_id=1, source_target_pairs={{0,1},{1,2},{2,3},{3,0},{4,5},{5,6},{6,7},{7,4},{8,9},{9,10},{10,1... | collective-permute-start | bytes 147464 | tf_op jit(solution)/shard_map/ppermute | solution.py:25
  10.7 11.6 %collective-permute-start.5 = (f32[3,1,4,8,128]{4,3,2,1,0:T(8,128)S(1)}, f32[3,1,4,8,128]{4,3,2,1,0:T(8,128)S(1)}, u32[]{:S(2)}, u32[]{:S(2)}) collective-permute-start(f32[3,1,4,8,128]{4,3,2,1,0:T(8,128)S(1)} %pad_maximum_fusion), channel_id=1, source_target_pairs={{1,0},{2,1},{3,2},{0,3},{5,4},{6,5},{7,6},{4,7},{9,8},{10,9},{11,1... | collective-permute-start | bytes 147464 | tf_op jit(solution)/shard_map/ppermute | solution.py:28
  45.5 3.1 %collective-permute-start.6 = (f32[2,1,2,1,128]{4,3,2,1,0:T(1,128)S(1)}, f32[2,1,2,1,128]{4,3,2,1,0:T(1,128)S(1)}, u32[]{:S(2)}, u32[]{:S(2)}) collective-permute-start(f32[2,1,2,1,128]{4,3,2,1,0:T(1,128)S(1)} %slice.2752), channel_id=1, source_target_pairs={{0,8},{8,16},{16,24},{24,0},{1,9},{9,17},{17,25},{25,1},{2,10},{10... | collective-permute-start | bytes 6152 | tf_op jit(solution)/shard_map/ppermute | solution.py:25
  48.5 1.3 %collective-permute-start.7 = (f32[2,1,2,1,128]{4,3,2,1,0:T(1,128)S(1)}, f32[2,1,2,1,128]{4,3,2,1,0:T(1,128)S(1)}, u32[]{:S(2)}, u32[]{:S(2)}) collective-permute-start(f32[2,1,2,1,128]{4,3,2,1,0:T(1,128)S(1)} %get-tuple-element.961), channel_id=1, source_target_pairs={{8,0},{16,8},{24,16},{0,24},{9,1},{17,9},{25,17},{1,25},{10,2},{18... | collective-permute-start | bytes 6152 | tf_op jit(solution)/shard_map/ppermute | solution.py:28
  49.9 3.8 %collective-permute-start.10 = (f32[1,1,8,128]{3,2,1,0:T(8,128)S(1)}, f32[1,1,8,128]{3,2,1,0:T(8,128)S(1)}, u32[]{:S(2)}, u32[]{:S(2)}) collective-permute-start(f32[1,1,8,128]{3,2,1,0:T(8,128)S(1)} %get-tuple-element.997), channel_id=1, source_target_pairs={{4,0},{0,4},{5,1},{1,5},{6,2},{2,6},{7,3},{3,7},{12,8},{8,12},{13,... | collective-permute-start | bytes 12296 | tf_op jit(solution)/shard_map/ppermute | solution.py:28
  51.5 3.6 %collective-permute-start.9 = (f32[1,1,8,128]{3,2,1,0:T(8,128)S(1)}, f32[1,1,8,128]{3,2,1,0:T(8,128)S(1)}, u32[]{:S(2)}, u32[]{:S(2)}) collective-permute-start(f32[1,1,8,128]{3,2,1,0:T(8,128)S(1)} %get-tuple-element.996), channel_id=1, source_target_pairs={{0,4},{4,0},{1,5},{5,1},{2,6},{6,2},{3,7},{7,3},{8,12},{12,8},{9,1... | collective-permute-start | bytes 12296 | tf_op jit(solution)/shard_map/ppermute | solution.py:25
  52.0 6.9 %collective-permute-start.8 = (f32[1,2,1,128]{3,2,1,0:T(1,128)S(1)}, f32[1,2,1,128]{3,2,1,0:T(1,128)S(1)}, u32[]{:S(2)}, u32[]{:S(2)}) collective-permute-start(f32[1,2,1,128]{3,2,1,0:T(1,128)S(1)} %get-tuple-element.995), channel_id=1, source_target_pairs={{0,8},{8,16},{16,24},{24,0},{1,9},{9,17},{17,25},{25,1},{2,10},{10... | collective-permute-start | bytes 3080 | tf_op jit(solution)/shard_map/ppermute | solution.py:25
  52.6 6.3 %collective-permute-start.12 = (f32[1,2,1,128]{3,2,1,0:T(1,128)S(1)}, f32[1,2,1,128]{3,2,1,0:T(1,128)S(1)}, u32[]{:S(2)}, u32[]{:S(2)}) collective-permute-start(f32[1,2,1,128]{3,2,1,0:T(1,128)S(1)} %get-tuple-element.994), channel_id=1, source_target_pairs={{8,0},{16,8},{24,16},{0,24},{9,1},{17,9},{25,17},{1,25},{10,2},{18... | collective-permute-start | bytes 3080 | tf_op jit(solution)/shard_map/ppermute | solution.py:28
  55.1 5.5 %collective-permute-start.11 = (f32[1,4,8,128]{3,2,1,0:T(8,128)S(1)}, f32[1,4,8,128]{3,2,1,0:T(8,128)S(1)}, u32[]{:S(2)}, u32[]{:S(2)}) collective-permute-start(f32[1,4,8,128]{3,2,1,0:T(8,128)S(1)} %pad_maximum_fusion.1), channel_id=1, source_target_pairs={{0,1},{1,2},{2,3},{3,0},{4,5},{5,6},{6,7},{7,4},{8,9},{9,10},{10,1... | collective-permute-start | bytes 49160 | tf_op jit(solution)/shard_map/ppermute | solution.py:25
  55.1 19.7 %collective-permute-start.13 = (f32[1,4,8,128]{3,2,1,0:T(8,128)S(1)}, f32[1,4,8,128]{3,2,1,0:T(8,128)S(1)}, u32[]{:S(2)}, u32[]{:S(2)}) collective-permute-start(f32[1,4,8,128]{3,2,1,0:T(8,128)S(1)} %pad_maximum_fusion.1), channel_id=1, source_target_pairs={{1,0},{2,1},{3,2},{0,3},{5,4},{6,5},{7,6},{4,7},{9,8},{10,9},{11,1... | collective-permute-start | bytes 49160 | tf_op jit(solution)/shard_map/ppermute | solution.py:28
  113.7 3.1 %collective-permute-start.14 = (f32[3,1,2,1,128]{4,3,2,1,0:T(1,128)S(1)}, f32[3,1,2,1,128]{4,3,2,1,0:T(1,128)S(1)}, u32[]{:S(2)}, u32[]{:S(2)}) collective-permute-start(f32[3,1,2,1,128]{4,3,2,1,0:T(1,128)S(1)} %slice.2795), channel_id=1, source_target_pairs={{0,8},{8,16},{16,24},{24,0},{1,9},{9,17},{17,25},{25,1},{2,10},{10... | collective-permute-start | bytes 9224 | tf_op jit(solution)/shard_map/ppermute | solution.py:25
  116.8 1.4 %collective-permute-start.15 = (f32[3,1,2,1,128]{4,3,2,1,0:T(1,128)S(1)}, f32[3,1,2,1,128]{4,3,2,1,0:T(1,128)S(1)}, u32[]{:S(2)}, u32[]{:S(2)}) collective-permute-start(f32[3,1,2,1,128]{4,3,2,1,0:T(1,128)S(1)} %get-tuple-element.935), channel_id=1, source_target_pairs={{8,0},{16,8},{24,16},{0,24},{9,1},{17,9},{25,17},{1,25},{10,2},{18... | collective-permute-start | bytes 9224 | tf_op jit(solution)/shard_map/ppermute | solution.py:28
where the time goes:
time: 120 us; the launch traced here: 119 us
  other arithmetic  79.3 us (66%)
  waiting for transfers between devices  15.8 us (13%)
  starting transfers between devices  15.6 us (13%)
  local copies, waits for them, and re-layouts  6.11 us (5%)
  between operations  1.92 us (2%)
    reduce_sum x8, other arithmetic, force_terms(): jnp.sum(factor * delta, -1)  49.1 us
    reduce_sum x3, other arithmetic, density_terms(): jnp.sum(square, -1)  27.4 us
    ppermute x8, waiting for transfers between devices, with_halo(): lax.ppermute(lax.slice_in_dim(block, block.shape[dim] - width, None, axis...  13.9 us
    ppermute x8, starting transfers between devices, with_halo(): lax.ppermute(lax.slice_in_dim(block, 0, width, axis=dim), axis, backward)  12.7 us
    ppermute x8, starting transfers between devices, with_halo(): lax.ppermute(lax.slice_in_dim(block, block.shape[dim] - width, None, axis...  2.96 us
    scatter-add x18, local copies, waits for them, and re-layouts, per_device(): pushes.at[:, :, :, 1 + step_z:1 + step_z + layers]  2.95 us
  transfers between devices with their start and end apart: 16, of which 8 were waited for; matrix products, arithmetic and copies ran while one was open for 19% of the time, Pallas kernels for 0%

commit v1 on v0

v1 whole, which is shorter than its diff:
```python
import functools

import jax
import jax.numpy as jnp
from jax import lax
from jax.experimental import pallas as pl
from jax.experimental.pallas import tpu as pltpu
from jax.sharding import PartitionSpec as P

SENTINEL = 4.0
PAIR_SCALE = 0.02
EMBED_SCALE = 0.2
CUTOFF_SQUARED = 0.25
FORCE_SCALE = 8.0
FAR = -1.0e6
ROWS = 8


def with_halo(block, sides, width):
    for axis, dim in sides:
        count = lax.axis_size(axis)
        forward = [(i, (i + 1) % count) for i in range(count)]
        backward = [(target, source) for source, target in forward]
        low = lax.ppermute(
            lax.slice_in_dim(block, block.shape[dim] - width, None, axis=dim), axis, forward
        )
        high = lax.ppermute(lax.slice_in_dim(block, 0, width, axis=dim), axis, backward)
        block = jnp.concatenate([low, block, high], axis=dim)
    return block


def split(value):
    first = value.astype(jnp.bfloat16).astype(jnp.float32)
    rest = value - first
    second = rest.astype(jnp.bfloat16).astype(jnp.float32)
    return first, second, rest - second


def far_rows(tile):
    b1, b2, b3 = split(tile)
    return jnp.concatenate([b1, b2, b1, b2, b3, b1], axis=0)


def own_rows(tile):
    a1, a2, a3 = split(tile)
    return jnp.concatenate([a1, a1, a2, a2, a1, a3], axis=0)


def place(index, sizes):
    return index // (sizes[1] * sizes[2]), index // sizes[2] % sizes[1], index % sizes[2]


def density_kernel(far_ref, own_ref, out_ref, turned):
    wide = far_ref.shape[:3]
    sizes = own_ref.shape[:3]
    slots = far_ref.shape[-1]

    def prepare(index, carry):
        x, y, z = place(index, wide)
        turned[x, y, z] = far_rows(far_ref[x, y, z]).T.astype(jnp.bfloat16)
        return carry

    lax.fori_loop(0, wide[0] * wide[1] * wide[2], prepare, 0, unroll=4)

    def cell(index, carry):
        x, y, z = place(index, sizes)
        own = own_rows(own_ref[x, y, z]).astype(jnp.bfloat16)
        rho = jnp.zeros((ROWS, slots), jnp.float32)
        quartic = jnp.zeros((ROWS, slots), jnp.float32)
        for dx in range(3):
            for dy in range(3):
                for dz in range(3):
                    w = jnp.dot(
                        turned[x + dx, y + dy, z + dz], own, preferred_element_type=jnp.float32
                    )
                    w = jnp.maximum(w, 0.0)
                    s = w * w
                    q = s * s
                    rho = rho + jnp.sum(s.reshape(-1, ROWS, slots), axis=0)
                    quartic = quartic + jnp.sum(q.reshape(-1, ROWS, slots), axis=0)
        rho = jnp.sum(rho, axis=0, keepdims=True) - 1.0
        quartic = jnp.sum(quartic, axis=0, keepdims=True) - 1.0
        row = lax.broadcasted_iota(jnp.int32, (ROWS, slots), 0)
        out_ref[x, y, z] = jnp.where(row == 0, rho, quartic)
        return carry

    lax.fori_loop(0, sizes[0] * sizes[1] * sizes[2], cell, 0)


def force_kernel(far_ref, own_ref, gain_ref, out_ref, turned, flat):
    wide = far_ref.shape[:3]
    sizes = own_ref.shape[:3]
    slots = far_ref.shape[-1]

    def prepare(index, carry):
        x, y, z = place(index, wide)
        b1, b2, b3 = split(far_ref[x, y, z])
        turned[x, y, z] = jnp.concatenate([b1, b2, b1, b2, b3, b1], axis=0).T.astype(jnp.bfloat16)
        flat[x, y, z] = jnp.concatenate([b1, b2, b3, jnp.zeros_like(b1)], axis=0).astype(
            jnp.bfloat16
        )
        return carry

    lax.fori_loop(0, wide[0] * wide[1] * wide[2], prepare, 0, unroll=4)

    def cell(index, carry):
        x, y, z = place(index, sizes)
        tile = own_ref[x, y, z]
        own = jnp.concatenate([own_rows(tile), own_rows(gain_ref[x, y, z])], axis=1).astype(
            jnp.bfloat16
        )
        total = jnp.zeros((4 * ROWS, slots), jnp.float32)
        for dx in range(3):
            for dy in range(3):
                for dz in range(3):
                    both = jnp.dot(
                        turned[x + dx, y + dy, z + dz], own, preferred_element_type=jnp.float32
                    )
                    w = jnp.maximum(both[:, :slots], 0.0)
                    f = w * (both[:, slots:] - w * w)
                    high = f.astype(jnp.bfloat16)
                    low = (f - high.astype(jnp.float32)).astype(jnp.bfloat16)
                    rows = flat[x + dx, y + dy, z + dz]
                    total = total + jnp.dot(rows, high, preferred_element_type=jnp.float32)
                    total = total + jnp.dot(rows, low, preferred_element_type=jnp.float32)
        total = total[:ROWS] + total[ROWS : 2 * ROWS] + total[2 * ROWS : 3 * ROWS]
        scale = FORCE_SCALE * 4.0 * PAIR_SCALE
        out_ref[x, y, z] = scale * (total - 0.125 * tile * total[4:5])
        return carry

    lax.fori_loop(0, sizes[0] * sizes[1] * sizes[2], cell, 0)


def per_device(positions, counts):
    slots = positions.shape[-1]
    sizes = positions.shape[1:4]
    wide = tuple(size + 2 for size in sizes)
    occupied = jnp.arange(slots, dtype=jnp.int32) < counts[..., None]
    seated = jnp.where(occupied[None], positions, SENTINEL)
    block = with_halo(seated, (("gz", 3), ("gy", 2), ("gx", 1)), 1)
    filled = block[0] < 2.0
    coords = []
    for component in range(3):
        steps = lax.broadcasted_iota(jnp.float32, wide, component) - 0.5 * wide[component]
        coords.append(jnp.where(filled, block[component] + steps[..., None], 0.0))
    near = 4.0 * (coords[0] * coords[0] + coords[1] * coords[1] + coords[2] * coords[2])
    one = jnp.ones_like(near)
    zero = jnp.zeros_like(near)
    inner = tuple(slice(1, 1 + size) for size in sizes)
    far_density = jnp.stack(
        coords + [jnp.where(filled, -near, FAR), one, zero, zero, zero], axis=3
    )
    own = jnp.stack(
        [8.0 * c[inner] for c in coords]
        + [one[inner], 1.0 - near[inner], zero[inner], zero[inner], zero[inner]],
        axis=3,
    )
    depth = 6 * ROWS
    sums = pl.pallas_call(
        density_kernel,
        out_shape=jax.ShapeDtypeStruct(sizes + (ROWS, slots), jnp.float32),
        in_specs=[pl.BlockSpec(memory_space=pltpu.VMEM)] * 2,
        out_specs=pl.BlockSpec(memory_space=pltpu.VMEM),
        scratch_shapes=[pltpu.VMEM(wide + (slots, depth), jnp.bfloat16)],
        name="density",
    )(far_density, own)
    rho_sum = jnp.where(occupied, sums[..., 0, :], 0.0)
    pair_sum = PAIR_SCALE * (sums[..., 1, :] - 2.0 * rho_sum)
    fprime = -0.5 * EMBED_SCALE * lax.rsqrt(rho_sum + 1.0)
    gain = 0.5 - fprime * (0.5 / PAIR_SCALE)
    gain_block = with_halo(gain, (("gz", 2), ("gy", 1), ("gx", 0)), 1)
    far_force = jnp.stack(
        coords + [jnp.where(filled, -near, FAR), one, gain_block, zero, zero], axis=3
    )
    pad = zero[inner]
    gain_own = jnp.stack([pad, pad, pad, pad, gain, one[inner], pad, pad], axis=3)
    pushes = pl.pallas_call(
        force_kernel,
        out_shape=jax.ShapeDtypeStruct(sizes + (ROWS, slots), jnp.float32),
        in_specs=[pl.BlockSpec(memory_space=pltpu.VMEM)] * 3,
        out_specs=pl.BlockSpec(memory_space=pltpu.VMEM),
        scratch_shapes=[
            pltpu.VMEM(wide + (slots, depth), jnp.bfloat16),
            pltpu.VMEM(wide + (4 * ROWS, slots), jnp.bfloat16),
        ],
        name="force",
    )(far_force, own, gain_own)
    energy = jnp.where(occupied, -EMBED_SCALE * jnp.sqrt(rho_sum + 1.0) + 0.5 * pair_sum, 0.0)
    forces = jnp.moveaxis(pushes[..., :3, :], 3, 0)
    forces = jnp.where(occupied[None], forces, 0.0)
    return (energy, forces)


def solution(mesh):
    placed = (P(None, "gx", "gy", "gz", None), P("gx", "gy", "gz"))
    return jax.shard_map(
        per_device,
        mesh=mesh,
        in_specs=placed,
        out_specs=(P("gx", "gy", "gz", None), P(None, "gx", "gy", "gz", None)),
        check_vma=False,
    )
```

time: 120 us -> 81 us (0.68)
  other arithmetic: 79.3 us -> 4.46 us
  Pallas kernels: 0 us -> 39.4 us
  waiting for transfers between devices: 15.8 us -> 14.3 us
    reduce_sum x11 -> x0, other arithmetic: 76.5 us -> none  [the longest x8 49.1 us: force_terms(): jnp.sum(factor * delta, -1)]
    pallas_call x0 -> x2, Pallas kernels: none -> 39.4 us  [the longest x1 25.7 us: per_device(): pl.pallas_call(force_kernel, out_shape=jax.ShapeDtypeStruct(sizes + (ROWS...]
    scatter-add x40 -> x0, local copies, waits for them, and re-layouts: 5.38 us -> none  [the longest x18 2.95 us: per_device(): pushes.at[:, :, :, 1 + step_z:1 + step_z + layers]]
    another operation x0 -> x11, local copies, waits for them, and re-layouts: none -> 3.59 us  [the longest x2 1.43 us: per_device(): jnp.stack(coords + [jnp.where(filled, -near, FAR), one, gain_block, zero,...]
    ppermute x8 -> x6, starting transfers between devices: 2.96 us -> 6.42 us  [with_halo(): lax.ppermute(lax.slice_in_dim(block, block.shape[dim] - width, None, axis...]
    ppermute x8 -> x6, waiting for transfers between devices: 13.9 us -> 10.5 us  [with_halo(): lax.ppermute(lax.slice_in_dim(block, block.shape[dim] - width, None, axis...]
    ppermute x8 -> x6, starting transfers between devices: 12.7 us -> 10.1 us  [with_halo(): lax.ppermute(lax.slice_in_dim(block, 0, width, axis=dim), axis, backward)]
    ppermute x8 -> x6, waiting for transfers between devices: 1.87 us -> 3.79 us  [with_halo(): lax.ppermute(lax.slice_in_dim(block, 0, width, axis=dim), axis, backward)]
  transfers between devices with their start and end apart: 16 -> 12, of which waited for: 8 -> 10; matrix products, arithmetic and copies ran while one was open for 19% -> 1% of each run, Pallas kernels for 0% -> 0%
where the time goes in v1:
time: 81 us; the launch traced here: 80.6 us
  Pallas kernels  39.4 us (49%)
  starting transfers between devices  16.5 us (20%)
  waiting for transfers between devices  14.3 us (18%)
  local copies, waits for them, and re-layouts  5.19 us (6%)
  other arithmetic  4.46 us (6%)
    pallas_call x1, Pallas kernels, per_device(): pl.pallas_call(force_kernel, out_shape=jax.ShapeDtypeStruct(sizes + (ROWS...  25.7 us
    pallas_call x1, Pallas kernels, per_device(): pl.pallas_call(density_kernel, out_shape=jax.ShapeDtypeStruct(sizes + (RO...  13.6 us
    ppermute x6, waiting for transfers between devices, with_halo(): lax.ppermute(lax.slice_in_dim(block, block.shape[dim] - width, None, axis...  10.5 us
    ppermute x6, starting transfers between devices, with_halo(): lax.ppermute(lax.slice_in_dim(block, 0, width, axis=dim), axis, backward)  10.1 us
    ppermute x6, starting transfers between devices, with_halo(): lax.ppermute(lax.slice_in_dim(block, block.shape[dim] - width, None, axis...  6.42 us
    ppermute x6, waiting for transfers between devices, with_halo(): lax.ppermute(lax.slice_in_dim(block, 0, width, axis=dim), axis, backward)  3.79 us
    sub x2, other arithmetic, per_device(): gain = 0.5 - fprime * (0.5 / PAIR_SCALE)  1.69 us
  transfers between devices with their start and end apart: 12, of which 10 were waited for; matrix products, arithmetic and copies ran while one was open for 1% of the time, Pallas kernels for 0%

profile of v1, /device:TPU:0, one launch (start us, length us, event | category | flops | bytes accessed | tf_op | source)
XLA Modules:
  0.0 80.6 jit_solution(84743885538720628)
XLA Ops:
  0.6 0.0 copy-start
  0.6 0.7 copy-done
  1.3 0.1 iota_compare_fusion
  1.4 0.7 broadcast_select_fusion
  2.1 0.5 collective-permute-start
  2.7 2.0 %collective-permute-start.1 = (f32[3,1,2,1,128]{4,3,2,1,0:T(1,128)S(1)}, f32[3,1,2,1,128]{4,3,2,1,0:T(1,128)S(1)}, u32[]{:S(2)}, u32[]{:S(2)}) collective-permute-start(f32[3,1,2,1,128]{4,3,2,1,0:T(1,128)S(1)} %get-tuple-element.24), channel_id=1, source_target_pairs={{8,0},{16,8},{24,16},{0,24},{9,1},{17,9},{25,17},{1,25},{10,2},{18... | collective-permute-start | bytes 9224 | tf_op jit(solution)/shard_map/ppermute | solution.py:27
  4.7 1.2 %collective-permute-done = f32[3,1,2,1,128]{4,3,2,1,0:T(1,128)S(1)} collective-permute-done((f32[3,1,2,1,128]{4,3,2,1,0:T(1,128)S(1)}, f32[3,1,2,1,128]{4,3,2,1,0:T(1,128)S(1)}, u32[]{:S(2)}, u32[]{:S(2)}) %collective-permute-start) | collective-permute-done | bytes 3104 | tf_op jit(solution)/shard_map/ppermute | solution.py:24
  5.9 0.1 collective-permute-done.1
  6.0 2.3 %collective-permute-start.2 = (f32[3,1,1,10,128]{4,3,2,1,0:T(8,128)S(1)}, f32[3,1,1,10,128]{4,3,2,1,0:T(8,128)S(1)}, u32[]{:S(2)}, u32[]{:S(2)}) collective-permute-start(f32[3,1,1,10,128]{4,3,2,1,0:T(8,128)S(1)} %get-tuple-element.21), channel_id=1, source_target_pairs={{0,4},{4,0},{1,5},{5,1},{2,6},{6,2},{3,7},{7,3},{8,12},{12,8},{9,1... | collective-permute-start | bytes 46088 | tf_op jit(solution)/shard_map/ppermute | solution.py:24
  8.3 0.1 collective-permute-start.3
  8.4 1.7 %collective-permute-done.2 = f32[3,1,1,10,128]{4,3,2,1,0:T(8,128)S(1)} collective-permute-done((f32[3,1,1,10,128]{4,3,2,1,0:T(8,128)S(1)}, f32[3,1,1,10,128]{4,3,2,1,0:T(8,128)S(1)}, u32[]{:S(2)}, u32[]{:S(2)}) %collective-permute-start.2) | collective-permute-done | bytes 15392 | tf_op jit(solution)/shard_map/ppermute | solution.py:24
  10.1 2.0 %collective-permute-done.3 = f32[3,1,1,10,128]{4,3,2,1,0:T(8,128)S(1)} collective-permute-done((f32[3,1,1,10,128]{4,3,2,1,0:T(8,128)S(1)}, f32[3,1,1,10,128]{4,3,2,1,0:T(8,128)S(1)}, u32[]{:S(2)}, u32[]{:S(2)}) %collective-permute-start.3) | collective-permute-done | bytes 15392 | tf_op jit(solution)/shard_map/ppermute | solution.py:27
  12.2 1.6 %collective-permute-start.4 = (f32[3,1,4,10,128]{4,3,2,1,0:T(8,128)S(1)}, f32[3,1,4,10,128]{4,3,2,1,0:T(8,128)S(1)}, u32[]{:S(2)}, u32[]{:S(2)}) collective-permute-start(f32[3,1,4,10,128]{4,3,2,1,0:T(8,128)S(1)} %pad_maximum_fusion.1), channel_id=1, source_target_pairs={{0,1},{1,2},{2,3},{3,0},{4,5},{5,6},{6,7},{7,4},{8,9},{9,10},{10,1... | collective-permute-start | bytes 184328 | tf_op jit(solution)/shard_map/ppermute | solution.py:24
  13.8 2.2 %collective-permute-start.5 = (f32[3,1,4,10,128]{4,3,2,1,0:T(8,128)S(1)}, f32[3,1,4,10,128]{4,3,2,1,0:T(8,128)S(1)}, u32[]{:S(2)}, u32[]{:S(2)}) collective-permute-start(f32[3,1,4,10,128]{4,3,2,1,0:T(8,128)S(1)} %pad_maximum_fusion.1), channel_id=1, source_target_pairs={{1,0},{2,1},{3,2},{0,3},{5,4},{6,5},{7,6},{4,7},{9,8},{10,9},{11,1... | collective-permute-start | bytes 184328 | tf_op jit(solution)/shard_map/ppermute | solution.py:27
  16.0 3.5 %collective-permute-done.4 = f32[3,1,4,10,128]{4,3,2,1,0:T(8,128)S(1)} collective-permute-done((f32[3,1,4,10,128]{4,3,2,1,0:T(8,128)S(1)}, f32[3,1,4,10,128]{4,3,2,1,0:T(8,128)S(1)}, u32[]{:S(2)}, u32[]{:S(2)}) %collective-permute-start.4) | collective-permute-done | bytes 61472 | tf_op jit(solution)/shard_map/ppermute | solution.py:24
  19.6 0.9 %collective-permute-done.5 = f32[3,1,4,10,128]{4,3,2,1,0:T(8,128)S(1)} collective-permute-done((f32[3,1,4,10,128]{4,3,2,1,0:T(8,128)S(1)}, f32[3,1,4,10,128]{4,3,2,1,0:T(8,128)S(1)}, u32[]{:S(2)}, u32[]{:S(2)}) %collective-permute-start.5) | collective-permute-done | bytes 61472 | tf_op jit(solution)/shard_map/ppermute | solution.py:27
  20.5 0.1 fusion
  20.6 0.1 negate_select_fusion
  20.7 0.1 fusion.1
  20.8 0.1 copy.20
  20.9 0.1 copy.21
  20.9 0.1 copy.22
  21.0 0.1 copy.23
  21.1 0.7 stack.48.own_ref
  22.0 1.4 %stack.42.far_ref = f32[3,4,10,8,128]{4,3,2,1,0:T(8,128)} concatenate(f32[3,4,10,1,128]{4,3,2,1,0:T(1,128)S(1)} %copy.20, f32[3,4,10,1,128]{4,3,2,1,0:T(1,128)S(1)} %copy.21, f32[3,4,10,1,128]{4,3,2,1,0:T(1,128)S(1)} %copy.22, f32[3,4,10,1,128]{4,3,2,1,0:T(1,128)S(1)} %copy.23, f32[3,4,10,1,128]{4,3,2,1,0:T(1,128)S(1)} %broadcast.272, ...), dimensions={3} | concatenate | bytes 983040 | tf_op jit(solution)/shard_map/stack | solution.py:150
  23.3 13.6 %density.1 = f32[1,2,8,8,128]{4,3,2,1,0:T(8,128)} custom-call(f32[3,4,10,8,128]{4,3,2,1,0:T(8,128)} %stack.42.far_ref, f32[1,2,8,8,128]{4,3,2,1,0:T(8,128)} %stack.48.own_ref), custom_call_target="tpu_custom_call" | custom-call | tf_op jit(solution)/shard_map/density/pallas_call | solution.py:159
  37.0 1.0 %multiply_subtract_fusion = (f32[1,2,8,1,128]{4,3,2,1,0:T(1,128)S(1)}, f32[1,2,8,1,128]{4,3,2,1,0:T(1,128)S(1)}, f32[1,2,8,1,128]{4,3,2,1,0:T(1,128)S(1)}) fusion(f32[1,2,8,1,128]{4,3,2,1,0:T(1,128)S(1)} %bitcast.53, s32[2,8]{1,0:T(2,128)S(1)} %bitcast.62, f32[1,2,8,8,128]{4,3,2,1,0:T(8,128)} %density.1), kind=kLoop, calls=%fused_computation.27 | loop fusion | flops 10240 | bytes 49216 | tf_op jit(solution)/shard_map/sub | solution.py:170
  38.0 0.7 multiply_subtract_fusion.1
  38.7 0.0 collective-permute-start.6
  38.7 1.7 %collective-permute-start.7 = (f32[1,2,1,128]{3,2,1,0:T(1,128)S(1)}, f32[1,2,1,128]{3,2,1,0:T(1,128)S(1)}, u32[]{:S(2)}, u32[]{:S(2)}) collective-permute-start(f32[1,2,1,128]{3,2,1,0:T(1,128)S(1)} %get-tuple-element.30), channel_id=1, source_target_pairs={{8,0},{16,8},{24,16},{0,24},{9,1},{17,9},{25,17},{1,25},{10,2},{18... | collective-permute-start | bytes 3080 | tf_op jit(solution)/shard_map/ppermute | solution.py:27
  40.4 1.3 %collective-permute-done.6 = f32[1,2,1,128]{3,2,1,0:T(1,128)S(1)} collective-permute-done((f32[1,2,1,128]{3,2,1,0:T(1,128)S(1)}, f32[1,2,1,128]{3,2,1,0:T(1,128)S(1)}, u32[]{:S(2)}, u32[]{:S(2)}) %collective-permute-start.6) | collective-permute-done | bytes 1056 | tf_op jit(solution)/shard_map/ppermute | solution.py:24
  41.7 0.0 collective-permute-done.7
  41.8 0.8 collective-permute-start.8
  42.5 1.3 %collective-permute-start.9 = (f32[1,1,10,128]{3,2,1,0:T(8,128)S(1)}, f32[1,1,10,128]{3,2,1,0:T(8,128)S(1)}, u32[]{:S(2)}, u32[]{:S(2)}) collective-permute-start(f32[1,1,10,128]{3,2,1,0:T(8,128)S(1)} %get-tuple-element.26), channel_id=1, source_target_pairs={{4,0},{0,4},{5,1},{1,5},{6,2},{2,6},{7,3},{3,7},{12,8},{8,12},{13,... | collective-permute-start | bytes 15368 | tf_op jit(solution)/shard_map/ppermute | solution.py:27
  43.9 1.6 %collective-permute-done.8 = f32[1,1,10,128]{3,2,1,0:T(8,128)S(1)} collective-permute-done((f32[1,1,10,128]{3,2,1,0:T(8,128)S(1)}, f32[1,1,10,128]{3,2,1,0:T(8,128)S(1)}, u32[]{:S(2)}, u32[]{:S(2)}) %collective-permute-start.8) | collective-permute-done | bytes 5152 | tf_op jit(solution)/shard_map/ppermute | solution.py:24
  45.5 0.7 collective-permute-done.9
  46.2 1.2 %collective-permute-start.10 = (f32[1,4,10,128]{3,2,1,0:T(8,128)S(1)}, f32[1,4,10,128]{3,2,1,0:T(8,128)S(1)}, u32[]{:S(2)}, u32[]{:S(2)}) collective-permute-start(f32[1,4,10,128]{3,2,1,0:T(8,128)S(1)} %pad_maximum_fusion.4), channel_id=1, source_target_pairs={{0,1},{1,2},{2,3},{3,0},{4,5},{5,6},{6,7},{7,4},{8,9},{9,10},{10,1... | collective-permute-start | bytes 61448 | tf_op jit(solution)/shard_map/ppermute | solution.py:24
  47.4 2.7 %collective-permute-start.11 = (f32[1,4,10,128]{3,2,1,0:T(8,128)S(1)}, f32[1,4,10,128]{3,2,1,0:T(8,128)S(1)}, u32[]{:S(2)}, u32[]{:S(2)}) collective-permute-start(f32[1,4,10,128]{3,2,1,0:T(8,128)S(1)} %pad_maximum_fusion.4), channel_id=1, source_target_pairs={{1,0},{2,1},{3,2},{0,3},{5,4},{6,5},{7,6},{4,7},{9,8},{10,9},{11,1... | collective-permute-start | bytes 61448 | tf_op jit(solution)/shard_map/ppermute | solution.py:27
  50.1 0.7 pad_maximum_fusion.2.gain_ref
  50.8 1.2 %collective-permute-done.10 = f32[1,4,10,128]{3,2,1,0:T(8,128)S(1)} collective-permute-done((f32[1,4,10,128]{3,2,1,0:T(8,128)S(1)}, f32[1,4,10,128]{3,2,1,0:T(8,128)S(1)}, u32[]{:S(2)}, u32[]{:S(2)}) %collective-permute-start.10) | collective-permute-done | bytes 20512 | tf_op jit(solution)/shard_map/ppermute | solution.py:24
  52.0 0.0 collective-permute-done.11
  52.0 0.1 copy.35
  52.1 1.4 %stack.50.far_ref = f32[3,4,10,8,128]{4,3,2,1,0:T(8,128)} concatenate(f32[3,4,10,1,128]{4,3,2,1,0:T(1,128)S(1)} %copy.20, f32[3,4,10,1,128]{4,3,2,1,0:T(1,128)S(1)} %copy.21, f32[3,4,10,1,128]{4,3,2,1,0:T(1,128)S(1)} %copy.22, f32[3,4,10,1,128]{4,3,2,1,0:T(1,128)S(1)} %copy.23, f32[3,4,10,1,128]{4,3,2,1,0:T(1,128)S(1)} %broadcast.272, f32[3,4,10,1,128]{4,3,2,1,0:T(1,128)S(1)} %copy.35, ...), dimensions={3} | concatenate | bytes 983040 | tf_op jit(solution)/shard_map/stack | solution.py:172
  53.4 25.7 %force.1 = f32[1,2,8,8,128]{4,3,2,1,0:T(8,128)} custom-call(f32[3,4,10,8,128]{4,3,2,1,0:T(8,128)} %stack.50.far_ref, f32[1,2,8,8,128]{4,3,2,1,0:T(8,128)} %stack.48.own_ref, f32[1,2,8,8,128]{4,3,2,1,0:T(8,128)} %pad_maximum_fusion.2.gain_ref), custom_call_target="tpu_custom_call" | custom-call | tf_op jit(solution)/shard_map/force/pallas_call | solution.py:177
  79.2 0.8 %fusion.6 = f32[3,1,2,8,128]{4,0,3,2,1:T(4,128)S(1)} fusion(f32[1,2,8,8,128]{4,3,2,1,0:T(8,128)} %force.1, pred[2,8,128]{2,1,0:T(8,128)(4,1)S(1)} %iota_compare_fusion), kind=kLoop, calls=%fused_computation.21 | loop fusion | flops 6144 | bytes 51200 | tf_op jit(solution)/shard_map/jit(_where)/select_n | solution.py:190
  80.0 0.6 copy.38
  (22 shorter events, 0.3 us)
Async XLA Ops:
  0.6 0.7 copy-start
  2.1 3.8 %collective-permute-start = (f32[3,1,2,1,128]{4,3,2,1,0:T(1,128)S(1)}, f32[3,1,2,1,128]{4,3,2,1,0:T(1,128)S(1)}, u32[]{:S(2)}, u32[]{:S(2)}) collective-permute-start(f32[3,1,2,1,128]{4,3,2,1,0:T(1,128)S(1)} %get-tuple-element.23), channel_id=1, source_target_pairs={{0,8},{8,16},{16,24},{24,0},{1,9},{9,17},{17,25},{25,1},{2,10},{10... | collective-permute-start | bytes 9224 | tf_op jit(solution)/shard_map/ppermute | solution.py:24
  2.7 3.3 %collective-permute-start.1 = (f32[3,1,2,1,128]{4,3,2,1,0:T(1,128)S(1)}, f32[3,1,2,1,128]{4,3,2,1,0:T(1,128)S(1)}, u32[]{:S(2)}, u32[]{:S(2)}) collective-permute-start(f32[3,1,2,1,128]{4,3,2,1,0:T(1,128)S(1)} %get-tuple-element.24), channel_id=1, source_target_pairs={{8,0},{16,8},{24,16},{0,24},{9,1},{17,9},{25,17},{1,25},{10,2},{18... | collective-permute-start | bytes 9224 | tf_op jit(solution)/shard_map/ppermute | solution.py:27
  6.0 4.1 %collective-permute-start.2 = (f32[3,1,1,10,128]{4,3,2,1,0:T(8,128)S(1)}, f32[3,1,1,10,128]{4,3,2,1,0:T(8,128)S(1)}, u32[]{:S(2)}, u32[]{:S(2)}) collective-permute-start(f32[3,1,1,10,128]{4,3,2,1,0:T(8,128)S(1)} %get-tuple-element.21), channel_id=1, source_target_pairs={{0,4},{4,0},{1,5},{5,1},{2,6},{6,2},{3,7},{7,3},{8,12},{12,8},{9,1... | collective-permute-start | bytes 46088 | tf_op jit(solution)/shard_map/ppermute | solution.py:24
  8.3 3.8 %collective-permute-start.3 = (f32[3,1,1,10,128]{4,3,2,1,0:T(8,128)S(1)}, f32[3,1,1,10,128]{4,3,2,1,0:T(8,128)S(1)}, u32[]{:S(2)}, u32[]{:S(2)}) collective-permute-start(f32[3,1,1,10,128]{4,3,2,1,0:T(8,128)S(1)} %get-tuple-element.22), channel_id=1, source_target_pairs={{4,0},{0,4},{5,1},{1,5},{6,2},{2,6},{7,3},{3,7},{12,8},{8,12},{13,... | collective-permute-start | bytes 46088 | tf_op jit(solution)/shard_map/ppermute | solution.py:27
  12.2 7.4 %collective-permute-start.4 = (f32[3,1,4,10,128]{4,3,2,1,0:T(8,128)S(1)}, f32[3,1,4,10,128]{4,3,2,1,0:T(8,128)S(1)}, u32[]{:S(2)}, u32[]{:S(2)}) collective-permute-start(f32[3,1,4,10,128]{4,3,2,1,0:T(8,128)S(1)} %pad_maximum_fusion.1), channel_id=1, source_target_pairs={{0,1},{1,2},{2,3},{3,0},{4,5},{5,6},{6,7},{7,4},{8,9},{9,10},{10,1... | collective-permute-start | bytes 184328 | tf_op jit(solution)/shard_map/ppermute | solution.py:24
  13.8 6.7 %collective-permute-start.5 = (f32[3,1,4,10,128]{4,3,2,1,0:T(8,128)S(1)}, f32[3,1,4,10,128]{4,3,2,1,0:T(8,128)S(1)}, u32[]{:S(2)}, u32[]{:S(2)}) collective-permute-start(f32[3,1,4,10,128]{4,3,2,1,0:T(8,128)S(1)} %pad_maximum_fusion.1), channel_id=1, source_target_pairs={{1,0},{2,1},{3,2},{0,3},{5,4},{6,5},{7,6},{4,7},{9,8},{10,9},{11,1... | collective-permute-start | bytes 184328 | tf_op jit(solution)/shard_map/ppermute | solution.py:27
  38.7 3.0 %collective-permute-start.6 = (f32[1,2,1,128]{3,2,1,0:T(1,128)S(1)}, f32[1,2,1,128]{3,2,1,0:T(1,128)S(1)}, u32[]{:S(2)}, u32[]{:S(2)}) collective-permute-start(f32[1,2,1,128]{3,2,1,0:T(1,128)S(1)} %get-tuple-element.29), channel_id=1, source_target_pairs={{0,8},{8,16},{16,24},{24,0},{1,9},{9,17},{17,25},{25,1},{2,10},{10... | collective-permute-start | bytes 3080 | tf_op jit(solution)/shard_map/ppermute | solution.py:24
  38.7 3.0 %collective-permute-start.7 = (f32[1,2,1,128]{3,2,1,0:T(1,128)S(1)}, f32[1,2,1,128]{3,2,1,0:T(1,128)S(1)}, u32[]{:S(2)}, u32[]{:S(2)}) collective-permute-start(f32[1,2,1,128]{3,2,1,0:T(1,128)S(1)} %get-tuple-element.30), channel_id=1, source_target_pairs={{8,0},{16,8},{24,16},{0,24},{9,1},{17,9},{25,17},{1,25},{10,2},{18... | collective-permute-start | bytes 3080 | tf_op jit(solution)/shard_map/ppermute | solution.py:27
  41.8 3.7 %collective-permute-start.8 = (f32[1,1,10,128]{3,2,1,0:T(8,128)S(1)}, f32[1,1,10,128]{3,2,1,0:T(8,128)S(1)}, u32[]{:S(2)}, u32[]{:S(2)}) collective-permute-start(f32[1,1,10,128]{3,2,1,0:T(8,128)S(1)} %get-tuple-element.25), channel_id=1, source_target_pairs={{0,4},{4,0},{1,5},{5,1},{2,6},{6,2},{3,7},{7,3},{8,12},{12,8},{9,1... | collective-permute-start | bytes 15368 | tf_op jit(solution)/shard_map/ppermute | solution.py:24
  42.5 3.7 %collective-permute-start.9 = (f32[1,1,10,128]{3,2,1,0:T(8,128)S(1)}, f32[1,1,10,128]{3,2,1,0:T(8,128)S(1)}, u32[]{:S(2)}, u32[]{:S(2)}) collective-permute-start(f32[1,1,10,128]{3,2,1,0:T(8,128)S(1)} %get-tuple-element.26), channel_id=1, source_target_pairs={{4,0},{0,4},{5,1},{1,5},{6,2},{2,6},{7,3},{3,7},{12,8},{8,12},{13,... | collective-permute-start | bytes 15368 | tf_op jit(solution)/shard_map/ppermute | solution.py:27
  46.2 5.8 %collective-permute-start.10 = (f32[1,4,10,128]{3,2,1,0:T(8,128)S(1)}, f32[1,4,10,128]{3,2,1,0:T(8,128)S(1)}, u32[]{:S(2)}, u32[]{:S(2)}) collective-permute-start(f32[1,4,10,128]{3,2,1,0:T(8,128)S(1)} %pad_maximum_fusion.4), channel_id=1, source_target_pairs={{0,1},{1,2},{2,3},{3,0},{4,5},{5,6},{6,7},{7,4},{8,9},{9,10},{10,1... | collective-permute-start | bytes 61448 | tf_op jit(solution)/shard_map/ppermute | solution.py:24
  47.4 4.6 %collective-permute-start.11 = (f32[1,4,10,128]{3,2,1,0:T(8,128)S(1)}, f32[1,4,10,128]{3,2,1,0:T(8,128)S(1)}, u32[]{:S(2)}, u32[]{:S(2)}) collective-permute-start(f32[1,4,10,128]{3,2,1,0:T(8,128)S(1)} %pad_maximum_fusion.4), channel_id=1, source_target_pairs={{1,0},{2,1},{3,2},{0,3},{5,4},{6,5},{7,6},{4,7},{9,8},{10,9},{11,1... | collective-permute-start | bytes 61448 | tf_op jit(solution)/shard_map/ppermute | solution.py:27

commit v2 on v1

--- a/solution.py
+++ b/solution.py
@@ -50,10 +50,39 @@
     return index // (sizes[1] * sizes[2]), index // sizes[2] % sizes[1], index % sizes[2]
 
 
+def groups(sizes):
+    depth = 2 if sizes[2] % 2 == 0 else 1
+    plan = []
+    for dx in range(3):
+        for jy in range(sizes[1] + 2):
+            for jz in range(depth + 2):
+                ys = [y for y in range(sizes[1]) if 0 <= jy - y <= 2]
+                zs = [z for z in range(depth) if 0 <= jz - z <= 2]
+                if len(ys) == sizes[1]:
+                    runs = [(True, [(y, z) for z in zs for y in ys])]
+                else:
+                    runs = [(False, [(y, z) for z in zs]) for y in ys]
+                plan.append((dx, jy, jz, runs))
+    return depth, plan
+
+
+def side_by_side(tiles, sizes, depth, layer_first):
+    order = (
+        [(y, z) for z in range(depth) for y in range(sizes[1])]
+        if layer_first
+        else [(y, z) for y in range(sizes[1]) for z in range(depth)]
+    )
+    return {key: at for at, key in enumerate(order)}, jnp.concatenate(
+        [tiles[key] for key in order], axis=1
+    )
+
+
 def density_kernel(far_ref, own_ref, out_ref, turned):
     wide = far_ref.shape[:3]
     sizes = own_ref.shape[:3]
     slots = far_ref.shape[-1]
+    depth, plan = groups(sizes)
+    keys = [(y, z) for y in range(sizes[1]) for z in range(depth)]
 
     def prepare(index, carry):
         x, y, z = place(index, wide)
@@ -62,73 +91,97 @@
 
     lax.fori_loop(0, wide[0] * wide[1] * wide[2], prepare, 0, unroll=4)
 
-    def cell(index, carry):
-        x, y, z = place(index, sizes)
-        own = own_rows(own_ref[x, y, z]).astype(jnp.bfloat16)
-        rho = jnp.zeros((ROWS, slots), jnp.float32)
-        quartic = jnp.zeros((ROWS, slots), jnp.float32)
-        for dx in range(3):
-            for dy in range(3):
-                for dz in range(3):
-                    w = jnp.dot(
-                        turned[x + dx, y + dy, z + dz], own, preferred_element_type=jnp.float32
-                    )
-                    w = jnp.maximum(w, 0.0)
+    def group(index, carry):
+        steps = sizes[2] // depth
+        x, z0 = index // steps, index % steps * depth
+        tiles = {
+            (y, z): own_rows(own_ref[x, y, z0 + z]).astype(jnp.bfloat16) for y, z in keys
+        }
+        packs = {flag: side_by_side(tiles, sizes, depth, flag) for flag in (True, False)}
+        rho = {key: jnp.zeros((ROWS, slots), jnp.float32) for key in keys}
+        quartic = {key: jnp.zeros((ROWS, slots), jnp.float32) for key in keys}
+        for dx, jy, jz, runs in plan:
+            rows = turned[x + dx, jy, z0 + jz]
+            for flag, targets in runs:
+                order, pack = packs[flag]
+                start = order[targets[0]] * slots
+                pack = pack[:, start : start + len(targets) * slots]
+                both = jnp.dot(rows, pack, preferred_element_type=jnp.float32)
+                for at, key in enumerate(targets):
+                    w = jnp.maximum(both[:, at * slots : (at + 1) * slots], 0.0)
                     s = w * w
                     q = s * s
-                    rho = rho + jnp.sum(s.reshape(-1, ROWS, slots), axis=0)
-                    quartic = quartic + jnp.sum(q.reshape(-1, ROWS, slots), axis=0)
-        rho = jnp.sum(rho, axis=0, keepdims=True) - 1.0
-        quartic = jnp.sum(quartic, axis=0, keepdims=True) - 1.0
+                    rho[key] = rho[key] + jnp.sum(s.reshape(-1, ROWS, slots), axis=0)
+                    quartic[key] = quartic[key] + jnp.sum(q.reshape(-1, ROWS, slots), axis=0)
         row = lax.broadcasted_iota(jnp.int32, (ROWS, slots), 0)
-        out_ref[x, y, z] = jnp.where(row == 0, rho, quartic)
-        return carry
-
-    lax.fori_loop(0, sizes[0] * sizes[1] * sizes[2], cell, 0)
-
-
-def force_kernel(far_ref, own_ref, gain_ref, out_ref, turned, flat):
+        for key in keys:
+            first = jnp.sum(rho[key], axis=0, keepdims=True) - 1.0
+            second = jnp.sum(quartic[key], axis=0, keepdims=True) - 1.0
+            out_ref[x, key[0], z0 + key[1]] = jnp.where(row == 0, first, second)
+        return carry
+
+    lax.fori_loop(0, sizes[0] * (sizes[2] // depth), group, 0)
+
+
+def force_kernel(far_ref, own_ref, gain_ref, out_ref, turned, flat, column):
     wide = far_ref.shape[:3]
     sizes = own_ref.shape[:3]
     slots = far_ref.shape[-1]
+    depth, plan = groups(sizes)
+    keys = [(y, z) for y in range(sizes[1]) for z in range(depth)]
 
     def prepare(index, carry):
         x, y, z = place(index, wide)
-        b1, b2, b3 = split(far_ref[x, y, z])
-        turned[x, y, z] = jnp.concatenate([b1, b2, b1, b2, b3, b1], axis=0).T.astype(jnp.bfloat16)
-        flat[x, y, z] = jnp.concatenate([b1, b2, b3, jnp.zeros_like(b1)], axis=0).astype(
-            jnp.bfloat16
-        )
+        tile = far_ref[x, y, z]
+        b1, b2, b3 = split(tile)
+        across = jnp.concatenate([b1, b2, b1, b2, b3, b1, tile], axis=0).T
+        turned[x, y, z] = across[:, : 6 * ROWS].astype(jnp.bfloat16)
+        column[x, y, z] = across[:, 6 * ROWS + 5 : 6 * ROWS + 6]
+        rows = jnp.concatenate([b1, b2, b3, jnp.zeros_like(b1)], axis=0).astype(jnp.bfloat16)
+        flat[x, y, z] = jnp.concatenate([rows, rows], axis=1)
         return carry
 
     lax.fori_loop(0, wide[0] * wide[1] * wide[2], prepare, 0, unroll=4)
 
-    def cell(index, carry):
-        x, y, z = place(index, sizes)
-        tile = own_ref[x, y, z]
-        own = jnp.concatenate([own_rows(tile), own_rows(gain_ref[x, y, z])], axis=1).astype(
-            jnp.bfloat16
-        )
-        total = jnp.zeros((4 * ROWS, slots), jnp.float32)
-        for dx in range(3):
-            for dy in range(3):
-                for dz in range(3):
-                    both = jnp.dot(
-                        turned[x + dx, y + dy, z + dz], own, preferred_element_type=jnp.float32
-                    )
-                    w = jnp.maximum(both[:, :slots], 0.0)
-                    f = w * (both[:, slots:] - w * w)
+    def group(index, carry):
+        steps = sizes[2] // depth
+        x, z0 = index // steps, index % steps * depth
+        tiles = {
+            (y, z): own_rows(own_ref[x, y, z0 + z]).astype(jnp.bfloat16) for y, z in keys
+        }
+        packs = {flag: side_by_side(tiles, sizes, depth, flag) for flag in (True, False)}
+        gains = {(y, z): gain_ref[x, y, z0 + z] for y, z in keys}
+        total = {key: jnp.zeros((4 * ROWS, slots), jnp.float32) for key in keys}
+        for dx, jy, jz, runs in plan:
+            rows = turned[x + dx, jy, z0 + jz]
+            moments = flat[x + dx, jy, z0 + jz]
+            far_gain = jnp.broadcast_to(column[x + dx, jy, z0 + jz], (slots, slots))
+            for flag, targets in runs:
+                order, pack = packs[flag]
+                start = order[targets[0]] * slots
+                pack = pack[:, start : start + len(targets) * slots]
+                both = jnp.dot(rows, pack, preferred_element_type=jnp.float32)
+                highs, lows = [], []
+                for at, key in enumerate(targets):
+                    w = jnp.maximum(both[:, at * slots : (at + 1) * slots], 0.0)
+                    f = w * ((far_gain + gains[key]) - w * w)
                     high = f.astype(jnp.bfloat16)
-                    low = (f - high.astype(jnp.float32)).astype(jnp.bfloat16)
-                    rows = flat[x + dx, y + dy, z + dz]
-                    total = total + jnp.dot(rows, high, preferred_element_type=jnp.float32)
-                    total = total + jnp.dot(rows, low, preferred_element_type=jnp.float32)
-        total = total[:ROWS] + total[ROWS : 2 * ROWS] + total[2 * ROWS : 3 * ROWS]
+                    highs.append(high)
+                    lows.append((f - high.astype(jnp.float32)).astype(jnp.bfloat16))
+                stacked = jnp.concatenate(
+                    [jnp.concatenate(highs, axis=1), jnp.concatenate(lows, axis=1)], axis=0
+                )
+                part = jnp.dot(moments, stacked, preferred_element_type=jnp.float32)
+                for at, key in enumerate(targets):
+                    total[key] = total[key] + part[:, at * slots : (at + 1) * slots]
         scale = FORCE_SCALE * 4.0 * PAIR_SCALE
-        out_ref[x, y, z] = scale * (total - 0.125 * tile * total[4:5])
-        return carry
-
-    lax.fori_loop(0, sizes[0] * sizes[1] * sizes[2], cell, 0)
+        for key in keys:
+            whole = total[key][:ROWS] + total[key][ROWS : 2 * ROWS] + total[key][2 * ROWS : 3 * ROWS]
+            tile = own_ref[x, key[0], z0 + key[1]]
+            out_ref[x, key[0], z0 + key[1]] = scale * (whole - 0.125 * tile * whole[4:5])
+        return carry
+
+    lax.fori_loop(0, sizes[0] * (sizes[2] // depth), group, 0)
 
 
 def per_device(positions, counts):
@@ -172,8 +225,7 @@
     far_force = jnp.stack(
         coords + [jnp.where(filled, -near, FAR), one, gain_block, zero, zero], axis=3
     )
-    pad = zero[inner]
-    gain_own = jnp.stack([pad, pad, pad, pad, gain, one[inner], pad, pad], axis=3)
+    gain_own = gain[..., None, :]
     pushes = pl.pallas_call(
         force_kernel,
         out_shape=jax.ShapeDtypeStruct(sizes + (ROWS, slots), jnp.float32),
@@ -181,7 +233,8 @@
         out_specs=pl.BlockSpec(memory_space=pltpu.VMEM),
         scratch_shapes=[
             pltpu.VMEM(wide + (slots, depth), jnp.bfloat16),
-            pltpu.VMEM(wide + (4 * ROWS, slots), jnp.bfloat16),
+            pltpu.VMEM(wide + (4 * ROWS, 2 * slots), jnp.bfloat16),
+            pltpu.VMEM(wide + (slots, 1), jnp.float32),
         ],
         name="force",
     )(far_force, own, gain_own)

time: 81 us -> 80.4 us (level)
  waiting for transfers between devices: 14.3 us -> 19.9 us
  Pallas kernels: 39.4 us -> 35.4 us
  starting transfers between devices: 16.5 us -> 14.5 us
    ppermute x6, waiting for transfers between devices: 3.79 us -> 8.02 us  [with_halo(): lax.ppermute(lax.slice_in_dim(block, 0, width, axis=dim), axis, backward)]
    pallas_call x1, Pallas kernels: 25.7 us -> 23.6 us  [per_device(): pl.pallas_call(force_kernel, out_shape=jax.ShapeDtypeStruct(sizes + (ROWS...]
    pallas_call x1, Pallas kernels: 13.6 us -> 11.7 us  [per_device(): pl.pallas_call(density_kernel, out_shape=jax.ShapeDtypeStruct(sizes + (RO...]
    ppermute x6, starting transfers between devices: 6.42 us -> 4.56 us  [with_halo(): lax.ppermute(lax.slice_in_dim(block, block.shape[dim] - width, None, axis...]
    ppermute x6, waiting for transfers between devices: 10.5 us -> 11.9 us  [with_halo(): lax.ppermute(lax.slice_in_dim(block, block.shape[dim] - width, None, axis...]
  transfers between devices with their start and end apart: 12 -> 12, of which waited for: 10 -> 11; matrix products, arithmetic and copies ran while one was open for 1% -> 0% of each run, Pallas kernels for 0% -> 0%
where the time goes in v2:
time: 80.4 us; the launch traced here: 80.1 us
  Pallas kernels  35.4 us (44%)
  waiting for transfers between devices  19.9 us (25%)
  starting transfers between devices  14.5 us (18%)
  local copies, waits for them, and re-layouts  5.18 us (6%)
  other arithmetic  4.35 us (5%)
    pallas_call x1, Pallas kernels, per_device(): pl.pallas_call(force_kernel, out_shape=jax.ShapeDtypeStruct(sizes + (ROWS...  23.6 us
    ppermute x6, waiting for transfers between devices, with_halo(): lax.ppermute(lax.slice_in_dim(block, block.shape[dim] - width, None, axis...  11.9 us
    pallas_call x1, Pallas kernels, per_device(): pl.pallas_call(density_kernel, out_shape=jax.ShapeDtypeStruct(sizes + (RO...  11.7 us
    ppermute x6, starting transfers between devices, with_halo(): lax.ppermute(lax.slice_in_dim(block, 0, width, axis=dim), axis, backward)  9.92 us
    ppermute x6, waiting for transfers between devices, with_halo(): lax.ppermute(lax.slice_in_dim(block, 0, width, axis=dim), axis, backward)  8.02 us
    ppermute x6, starting transfers between devices, with_halo(): lax.ppermute(lax.slice_in_dim(block, block.shape[dim] - width, None, axis...  4.56 us
    sub x2, other arithmetic, per_device(): gain = 0.5 - fprime * (0.5 / PAIR_SCALE)  2.29 us
  transfers between devices with their start and end apart: 12, of which 11 were waited for; matrix products, arithmetic and copies ran while one was open for 0% of the time, Pallas kernels for 0%

profile of v2, /device:TPU:0, one launch (start us, length us, event | category | flops | bytes accessed | tf_op | source)
XLA Modules:
  0.0 80.1 jit_solution(10787222191689190421)
XLA Ops:
  0.6 0.0 copy-start
  0.6 0.7 copy-done
  1.3 0.1 iota_compare_fusion
  1.4 0.7 broadcast_select_fusion
  2.1 0.5 collective-permute-start
  2.7 2.0 %collective-permute-start.1 = (f32[3,1,2,1,128]{4,3,2,1,0:T(1,128)S(1)}, f32[3,1,2,1,128]{4,3,2,1,0:T(1,128)S(1)}, u32[]{:S(2)}, u32[]{:S(2)}) collective-permute-start(f32[3,1,2,1,128]{4,3,2,1,0:T(1,128)S(1)} %get-tuple-element.24), channel_id=1, source_target_pairs={{8,0},{16,8},{24,16},{0,24},{9,1},{17,9},{25,17},{1,25},{10,2},{18... | collective-permute-start | bytes 9224 | tf_op jit(solution)/shard_map/ppermute | solution.py:27
  4.7 1.2 %collective-permute-done = f32[3,1,2,1,128]{4,3,2,1,0:T(1,128)S(1)} collective-permute-done((f32[3,1,2,1,128]{4,3,2,1,0:T(1,128)S(1)}, f32[3,1,2,1,128]{4,3,2,1,0:T(1,128)S(1)}, u32[]{:S(2)}, u32[]{:S(2)}) %collective-permute-start) | collective-permute-done | bytes 3104 | tf_op jit(solution)/shard_map/ppermute | solution.py:24
  5.9 0.1 collective-permute-done.1
  6.0 2.3 %collective-permute-start.2 = (f32[3,1,1,10,128]{4,3,2,1,0:T(8,128)S(1)}, f32[3,1,1,10,128]{4,3,2,1,0:T(8,128)S(1)}, u32[]{:S(2)}, u32[]{:S(2)}) collective-permute-start(f32[3,1,1,10,128]{4,3,2,1,0:T(8,128)S(1)} %get-tuple-element.21), channel_id=1, source_target_pairs={{0,4},{4,0},{1,5},{5,1},{2,6},{6,2},{3,7},{7,3},{8,12},{12,8},{9,1... | collective-permute-start | bytes 46088 | tf_op jit(solution)/shard_map/ppermute | solution.py:24
  8.3 0.1 collective-permute-start.3
  8.4 1.7 %collective-permute-done.2 = f32[3,1,1,10,128]{4,3,2,1,0:T(8,128)S(1)} collective-permute-done((f32[3,1,1,10,128]{4,3,2,1,0:T(8,128)S(1)}, f32[3,1,1,10,128]{4,3,2,1,0:T(8,128)S(1)}, u32[]{:S(2)}, u32[]{:S(2)}) %collective-permute-start.2) | collective-permute-done | bytes 15392 | tf_op jit(solution)/shard_map/ppermute | solution.py:24
  10.1 2.0 %collective-permute-done.3 = f32[3,1,1,10,128]{4,3,2,1,0:T(8,128)S(1)} collective-permute-done((f32[3,1,1,10,128]{4,3,2,1,0:T(8,128)S(1)}, f32[3,1,1,10,128]{4,3,2,1,0:T(8,128)S(1)}, u32[]{:S(2)}, u32[]{:S(2)}) %collective-permute-start.3) | collective-permute-done | bytes 15392 | tf_op jit(solution)/shard_map/ppermute | solution.py:27
  12.2 3.7 %collective-permute-start.5 = (f32[3,1,4,10,128]{4,3,2,1,0:T(8,128)S(1)}, f32[3,1,4,10,128]{4,3,2,1,0:T(8,128)S(1)}, u32[]{:S(2)}, u32[]{:S(2)}) collective-permute-start(f32[3,1,4,10,128]{4,3,2,1,0:T(8,128)S(1)} %pad_maximum_fusion.1), channel_id=1, source_target_pairs={{1,0},{2,1},{3,2},{0,3},{5,4},{6,5},{7,6},{4,7},{9,8},{10,9},{11,1... | collective-permute-start | bytes 184328 | tf_op jit(solution)/shard_map/ppermute | solution.py:27
  15.8 0.0 collective-permute-start.4
  15.8 3.2 %collective-permute-done.5 = f32[3,1,4,10,128]{4,3,2,1,0:T(8,128)S(1)} collective-permute-done((f32[3,1,4,10,128]{4,3,2,1,0:T(8,128)S(1)}, f32[3,1,4,10,128]{4,3,2,1,0:T(8,128)S(1)}, u32[]{:S(2)}, u32[]{:S(2)}) %collective-permute-start.5) | collective-permute-done | bytes 61472 | tf_op jit(solution)/shard_map/ppermute | solution.py:27
  19.1 3.2 %collective-permute-done.4 = f32[3,1,4,10,128]{4,3,2,1,0:T(8,128)S(1)} collective-permute-done((f32[3,1,4,10,128]{4,3,2,1,0:T(8,128)S(1)}, f32[3,1,4,10,128]{4,3,2,1,0:T(8,128)S(1)}, u32[]{:S(2)}, u32[]{:S(2)}) %collective-permute-start.4) | collective-permute-done | bytes 61472 | tf_op jit(solution)/shard_map/ppermute | solution.py:24
  22.3 0.1 fusion
  22.3 0.1 negate_select_fusion
  22.5 0.1 fusion.1
  22.6 0.1 copy.23
  22.6 0.1 copy.22
  22.7 0.1 copy.21
  22.8 0.1 copy.20
  22.9 0.7 stack.49.own_ref
  23.7 1.4 %stack.41.far_ref = f32[3,4,10,8,128]{4,3,2,1,0:T(8,128)} concatenate(f32[3,4,10,1,128]{4,3,2,1,0:T(1,128)S(1)} %copy.20, f32[3,4,10,1,128]{4,3,2,1,0:T(1,128)S(1)} %copy.21, f32[3,4,10,1,128]{4,3,2,1,0:T(1,128)S(1)} %copy.22, f32[3,4,10,1,128]{4,3,2,1,0:T(1,128)S(1)} %copy.23, f32[3,4,10,1,128]{4,3,2,1,0:T(1,128)S(1)} %broadcast.266, ...), dimensions={3} | concatenate | bytes 983040 | tf_op jit(solution)/shard_map/stack | solution.py:203
  25.1 11.7 %density.1 = f32[1,2,8,8,128]{4,3,2,1,0:T(8,128)} custom-call(f32[3,4,10,8,128]{4,3,2,1,0:T(8,128)} %stack.41.far_ref, f32[1,2,8,8,128]{4,3,2,1,0:T(8,128)} %stack.49.own_ref), custom_call_target="tpu_custom_call" | custom-call | tf_op jit(solution)/shard_map/density/pallas_call | solution.py:212
  36.8 1.6 %multiply_subtract_fusion = (f32[1,2,8,1,128]{4,3,2,1,0:T(1,128)}, f32[1,2,8,1,128]{4,3,2,1,0:T(1,128)S(1)}, f32[1,2,8,1,128]{4,3,2,1,0:T(1,128)S(1)}) fusion(f32[1,2,8,1,128]{4,3,2,1,0:T(1,128)S(1)} %bitcast.53, s32[2,8]{1,0:T(2,128)S(1)} %bitcast.61, f32[1,2,8,8,128]{4,3,2,1,0:T(8,128)} %density.1), kind=kLoop, calls=%fused_computation.26 | loop fusion | flops 10240 | bytes 49216 | tf_op jit(solution)/shard_map/sub | solution.py:223
  38.4 0.7 multiply_subtract_fusion.1
  39.1 0.0 collective-permute-start.6
  39.1 1.7 %collective-permute-start.7 = (f32[1,2,1,128]{3,2,1,0:T(1,128)S(1)}, f32[1,2,1,128]{3,2,1,0:T(1,128)S(1)}, u32[]{:S(2)}, u32[]{:S(2)}) collective-permute-start(f32[1,2,1,128]{3,2,1,0:T(1,128)S(1)} %get-tuple-element.30), channel_id=1, source_target_pairs={{8,0},{16,8},{24,16},{0,24},{9,1},{17,9},{25,17},{1,25},{10,2},{18... | collective-permute-start | bytes 3080 | tf_op jit(solution)/shard_map/ppermute | solution.py:27
  40.9 1.3 %collective-permute-done.6 = f32[1,2,1,128]{3,2,1,0:T(1,128)S(1)} collective-permute-done((f32[1,2,1,128]{3,2,1,0:T(1,128)S(1)}, f32[1,2,1,128]{3,2,1,0:T(1,128)S(1)}, u32[]{:S(2)}, u32[]{:S(2)}) %collective-permute-start.6) | collective-permute-done | bytes 1056 | tf_op jit(solution)/shard_map/ppermute | solution.py:24
  42.1 0.0 collective-permute-done.7
  42.2 0.8 %collective-permute-start.8 = (f32[1,1,10,128]{3,2,1,0:T(8,128)S(1)}, f32[1,1,10,128]{3,2,1,0:T(8,128)S(1)}, u32[]{:S(2)}, u32[]{:S(2)}) collective-permute-start(f32[1,1,10,128]{3,2,1,0:T(8,128)S(1)} %get-tuple-element.25), channel_id=1, source_target_pairs={{0,4},{4,0},{1,5},{5,1},{2,6},{6,2},{3,7},{7,3},{8,12},{12,8},{9,1... | collective-permute-start | bytes 15368 | tf_op jit(solution)/shard_map/ppermute | solution.py:24
  43.0 1.3 %collective-permute-start.9 = (f32[1,1,10,128]{3,2,1,0:T(8,128)S(1)}, f32[1,1,10,128]{3,2,1,0:T(8,128)S(1)}, u32[]{:S(2)}, u32[]{:S(2)}) collective-permute-start(f32[1,1,10,128]{3,2,1,0:T(8,128)S(1)} %get-tuple-element.26), channel_id=1, source_target_pairs={{4,0},{0,4},{5,1},{1,5},{6,2},{2,6},{7,3},{3,7},{12,8},{8,12},{13,... | collective-permute-start | bytes 15368 | tf_op jit(solution)/shard_map/ppermute | solution.py:27
  44.3 1.6 %collective-permute-done.8 = f32[1,1,10,128]{3,2,1,0:T(8,128)S(1)} collective-permute-done((f32[1,1,10,128]{3,2,1,0:T(8,128)S(1)}, f32[1,1,10,128]{3,2,1,0:T(8,128)S(1)}, u32[]{:S(2)}, u32[]{:S(2)}) %collective-permute-start.8) | collective-permute-done | bytes 5152 | tf_op jit(solution)/shard_map/ppermute | solution.py:24
  45.9 0.7 collective-permute-done.9
  46.6 1.2 %collective-permute-start.11 = (f32[1,4,10,128]{3,2,1,0:T(8,128)S(1)}, f32[1,4,10,128]{3,2,1,0:T(8,128)S(1)}, u32[]{:S(2)}, u32[]{:S(2)}) collective-permute-start(f32[1,4,10,128]{3,2,1,0:T(8,128)S(1)} %pad_maximum_fusion.3), channel_id=1, source_target_pairs={{1,0},{2,1},{3,2},{0,3},{5,4},{6,5},{7,6},{4,7},{9,8},{10,9},{11,1... | collective-permute-start | bytes 61448 | tf_op jit(solution)/shard_map/ppermute | solution.py:27
  47.8 0.9 %collective-permute-start.10 = (f32[1,4,10,128]{3,2,1,0:T(8,128)S(1)}, f32[1,4,10,128]{3,2,1,0:T(8,128)S(1)}, u32[]{:S(2)}, u32[]{:S(2)}) collective-permute-start(f32[1,4,10,128]{3,2,1,0:T(8,128)S(1)} %pad_maximum_fusion.3), channel_id=1, source_target_pairs={{0,1},{1,2},{2,3},{3,0},{4,5},{5,6},{6,7},{7,4},{8,9},{9,10},{10,1... | collective-permute-start | bytes 61448 | tf_op jit(solution)/shard_map/ppermute | solution.py:24
  48.7 1.9 %collective-permute-done.11 = f32[1,4,10,128]{3,2,1,0:T(8,128)S(1)} collective-permute-done((f32[1,4,10,128]{3,2,1,0:T(8,128)S(1)}, f32[1,4,10,128]{3,2,1,0:T(8,128)S(1)}, u32[]{:S(2)}, u32[]{:S(2)}) %collective-permute-start.11) | collective-permute-done | bytes 20512 | tf_op jit(solution)/shard_map/ppermute | solution.py:27
  50.6 2.9 %collective-permute-done.10 = f32[1,4,10,128]{3,2,1,0:T(8,128)S(1)} collective-permute-done((f32[1,4,10,128]{3,2,1,0:T(8,128)S(1)}, f32[1,4,10,128]{3,2,1,0:T(8,128)S(1)}, u32[]{:S(2)}, u32[]{:S(2)}) %collective-permute-start.10) | collective-permute-done | bytes 20512 | tf_op jit(solution)/shard_map/ppermute | solution.py:24
  53.5 0.1 copy.35
  53.6 1.4 %stack.51.far_ref = f32[3,4,10,8,128]{4,3,2,1,0:T(8,128)} concatenate(f32[3,4,10,1,128]{4,3,2,1,0:T(1,128)S(1)} %copy.20, f32[3,4,10,1,128]{4,3,2,1,0:T(1,128)S(1)} %copy.21, f32[3,4,10,1,128]{4,3,2,1,0:T(1,128)S(1)} %copy.22, f32[3,4,10,1,128]{4,3,2,1,0:T(1,128)S(1)} %copy.23, f32[3,4,10,1,128]{4,3,2,1,0:T(1,128)S(1)} %broadcast.266, f32[3,4,10,1,128]{4,3,2,1,0:T(1,128)S(1)} %copy.35, ...), dimensions={3} | concatenate | bytes 983040 | tf_op jit(solution)/shard_map/stack | solution.py:225
  55.0 23.6 %force.1 = f32[1,2,8,8,128]{4,3,2,1,0:T(8,128)} custom-call(f32[3,4,10,8,128]{4,3,2,1,0:T(8,128)} %stack.51.far_ref, f32[1,2,8,8,128]{4,3,2,1,0:T(8,128)} %stack.49.own_ref, f32[1,2,8,1,128]{4,3,2,1,0:T(1,128)} %get-tuple-element.18.gain_ref), custom_call_target="tpu_custom_call" | custom-call | tf_op jit(solution)/shard_map/force/pallas_call | solution.py:229
  78.6 0.8 %fusion.6 = f32[3,1,2,8,128]{4,0,3,2,1:T(4,128)S(1)} fusion(f32[1,2,8,8,128]{4,3,2,1,0:T(8,128)} %force.1, pred[2,8,128]{2,1,0:T(8,128)(4,1)S(1)} %iota_compare_fusion), kind=kLoop, calls=%fused_computation.20 | loop fusion | flops 6144 | bytes 51200 | tf_op jit(solution)/shard_map/jit(_where)/select_n | solution.py:243
  79.5 0.6 copy.37
  (20 shorter events, 0.3 us)
Async XLA Ops:
  0.6 0.7 copy-start
  2.1 3.8 %collective-permute-start = (f32[3,1,2,1,128]{4,3,2,1,0:T(1,128)S(1)}, f32[3,1,2,1,128]{4,3,2,1,0:T(1,128)S(1)}, u32[]{:S(2)}, u32[]{:S(2)}) collective-permute-start(f32[3,1,2,1,128]{4,3,2,1,0:T(1,128)S(1)} %get-tuple-element.23), channel_id=1, source_target_pairs={{0,8},{8,16},{16,24},{24,0},{1,9},{9,17},{17,25},{25,1},{2,10},{10... | collective-permute-start | bytes 9224 | tf_op jit(solution)/shard_map/ppermute | solution.py:24
  2.7 3.3 %collective-permute-start.1 = (f32[3,1,2,1,128]{4,3,2,1,0:T(1,128)S(1)}, f32[3,1,2,1,128]{4,3,2,1,0:T(1,128)S(1)}, u32[]{:S(2)}, u32[]{:S(2)}) collective-permute-start(f32[3,1,2,1,128]{4,3,2,1,0:T(1,128)S(1)} %get-tuple-element.24), channel_id=1, source_target_pairs={{8,0},{16,8},{24,16},{0,24},{9,1},{17,9},{25,17},{1,25},{10,2},{18... | collective-permute-start | bytes 9224 | tf_op jit(solution)/shard_map/ppermute | solution.py:27
  6.0 4.1 %collective-permute-start.2 = (f32[3,1,1,10,128]{4,3,2,1,0:T(8,128)S(1)}, f32[3,1,1,10,128]{4,3,2,1,0:T(8,128)S(1)}, u32[]{:S(2)}, u32[]{:S(2)}) collective-permute-start(f32[3,1,1,10,128]{4,3,2,1,0:T(8,128)S(1)} %get-tuple-element.21), channel_id=1, source_target_pairs={{0,4},{4,0},{1,5},{5,1},{2,6},{6,2},{3,7},{7,3},{8,12},{12,8},{9,1... | collective-permute-start | bytes 46088 | tf_op jit(solution)/shard_map/ppermute | solution.py:24
  8.3 3.8 %collective-permute-start.3 = (f32[3,1,1,10,128]{4,3,2,1,0:T(8,128)S(1)}, f32[3,1,1,10,128]{4,3,2,1,0:T(8,128)S(1)}, u32[]{:S(2)}, u32[]{:S(2)}) collective-permute-start(f32[3,1,1,10,128]{4,3,2,1,0:T(8,128)S(1)} %get-tuple-element.22), channel_id=1, source_target_pairs={{4,0},{0,4},{5,1},{1,5},{6,2},{2,6},{7,3},{3,7},{12,8},{8,12},{13,... | collective-permute-start | bytes 46088 | tf_op jit(solution)/shard_map/ppermute | solution.py:27
  12.2 6.9 %collective-permute-start.5 = (f32[3,1,4,10,128]{4,3,2,1,0:T(8,128)S(1)}, f32[3,1,4,10,128]{4,3,2,1,0:T(8,128)S(1)}, u32[]{:S(2)}, u32[]{:S(2)}) collective-permute-start(f32[3,1,4,10,128]{4,3,2,1,0:T(8,128)S(1)} %pad_maximum_fusion.1), channel_id=1, source_target_pairs={{1,0},{2,1},{3,2},{0,3},{5,4},{6,5},{7,6},{4,7},{9,8},{10,9},{11,1... | collective-permute-start | bytes 184328 | tf_op jit(solution)/shard_map/ppermute | solution.py:27
  15.8 6.4 %collective-permute-start.4 = (f32[3,1,4,10,128]{4,3,2,1,0:T(8,128)S(1)}, f32[3,1,4,10,128]{4,3,2,1,0:T(8,128)S(1)}, u32[]{:S(2)}, u32[]{:S(2)}) collective-permute-start(f32[3,1,4,10,128]{4,3,2,1,0:T(8,128)S(1)} %pad_maximum_fusion.1), channel_id=1, source_target_pairs={{0,1},{1,2},{2,3},{3,0},{4,5},{5,6},{6,7},{7,4},{8,9},{9,10},{10,1... | collective-permute-start | bytes 184328 | tf_op jit(solution)/shard_map/ppermute | solution.py:24
  39.1 3.0 %collective-permute-start.6 = (f32[1,2,1,128]{3,2,1,0:T(1,128)S(1)}, f32[1,2,1,128]{3,2,1,0:T(1,128)S(1)}, u32[]{:S(2)}, u32[]{:S(2)}) collective-permute-start(f32[1,2,1,128]{3,2,1,0:T(1,128)S(1)} %get-tuple-element.29), channel_id=1, source_target_pairs={{0,8},{8,16},{16,24},{24,0},{1,9},{9,17},{17,25},{25,1},{2,10},{10... | collective-permute-start | bytes 3080 | tf_op jit(solution)/shard_map/ppermute | solution.py:24
  39.1 3.0 %collective-permute-start.7 = (f32[1,2,1,128]{3,2,1,0:T(1,128)S(1)}, f32[1,2,1,128]{3,2,1,0:T(1,128)S(1)}, u32[]{:S(2)}, u32[]{:S(2)}) collective-permute-start(f32[1,2,1,128]{3,2,1,0:T(1,128)S(1)} %get-tuple-element.30), channel_id=1, source_target_pairs={{8,0},{16,8},{24,16},{0,24},{9,1},{17,9},{25,17},{1,25},{10,2},{18... | collective-permute-start | bytes 3080 | tf_op jit(solution)/shard_map/ppermute | solution.py:27
  42.2 3.7 %collective-permute-start.8 = (f32[1,1,10,128]{3,2,1,0:T(8,128)S(1)}, f32[1,1,10,128]{3,2,1,0:T(8,128)S(1)}, u32[]{:S(2)}, u32[]{:S(2)}) collective-permute-start(f32[1,1,10,128]{3,2,1,0:T(8,128)S(1)} %get-tuple-element.25), channel_id=1, source_target_pairs={{0,4},{4,0},{1,5},{5,1},{2,6},{6,2},{3,7},{7,3},{8,12},{12,8},{9,1... | collective-permute-start | bytes 15368 | tf_op jit(solution)/shard_map/ppermute | solution.py:24
  43.0 3.7 %collective-permute-start.9 = (f32[1,1,10,128]{3,2,1,0:T(8,128)S(1)}, f32[1,1,10,128]{3,2,1,0:T(8,128)S(1)}, u32[]{:S(2)}, u32[]{:S(2)}) collective-permute-start(f32[1,1,10,128]{3,2,1,0:T(8,128)S(1)} %get-tuple-element.26), channel_id=1, source_target_pairs={{4,0},{0,4},{5,1},{1,5},{6,2},{2,6},{7,3},{3,7},{12,8},{8,12},{13,... | collective-permute-start | bytes 15368 | tf_op jit(solution)/shard_map/ppermute | solution.py:27
  46.6 4.0 %collective-permute-start.11 = (f32[1,4,10,128]{3,2,1,0:T(8,128)S(1)}, f32[1,4,10,128]{3,2,1,0:T(8,128)S(1)}, u32[]{:S(2)}, u32[]{:S(2)}) collective-permute-start(f32[1,4,10,128]{3,2,1,0:T(8,128)S(1)} %pad_maximum_fusion.3), channel_id=1, source_target_pairs={{1,0},{2,1},{3,2},{0,3},{5,4},{6,5},{7,6},{4,7},{9,8},{10,9},{11,1... | collective-permute-start | bytes 61448 | tf_op jit(solution)/shard_map/ppermute | solution.py:27
  47.8 5.7 %collective-permute-start.10 = (f32[1,4,10,128]{3,2,1,0:T(8,128)S(1)}, f32[1,4,10,128]{3,2,1,0:T(8,128)S(1)}, u32[]{:S(2)}, u32[]{:S(2)}) collective-permute-start(f32[1,4,10,128]{3,2,1,0:T(8,128)S(1)} %pad_maximum_fusion.3), channel_id=1, source_target_pairs={{0,1},{1,2},{2,3},{3,0},{4,5},{5,6},{6,7},{7,4},{8,9},{9,10},{10,1... | collective-permute-start | bytes 61448 | tf_op jit(solution)/shard_map/ppermute | solution.py:24

commit v3 on v2

v3 whole, which is shorter than its diff:
```python
import functools

import jax
import jax.numpy as jnp
from jax import lax
from jax.experimental import pallas as pl
from jax.experimental.pallas import tpu as pltpu
from jax.sharding import PartitionSpec as P

SENTINEL = 4.0
PAIR_SCALE = 0.02
EMBED_SCALE = 0.2
CUTOFF_SQUARED = 0.25
FORCE_SCALE = 8.0
FAR = -1.0e6
ROWS = 8


def split(value):
    first = value.astype(jnp.bfloat16).astype(jnp.float32)
    rest = value - first
    second = rest.astype(jnp.bfloat16).astype(jnp.float32)
    return first, second, rest - second


def far_rows(tile):
    b1, b2, b3 = split(tile)
    return jnp.concatenate([b1, b2, b1, b2, b3, b1], axis=0)


def own_rows(tile):
    a1, a2, a3 = split(tile)
    return jnp.concatenate([a1, a1, a2, a2, a1, a3], axis=0)


def place(index, sizes):
    return index // (sizes[1] * sizes[2]), index // sizes[2] % sizes[1], index % sizes[2]


def groups(sizes):
    depth = 2 if sizes[2] % 2 == 0 else 1
    plan = []
    for dx in range(3):
        for jy in range(sizes[1] + 2):
            for jz in range(depth + 2):
                ys = [y for y in range(sizes[1]) if 0 <= jy - y <= 2]
                zs = [z for z in range(depth) if 0 <= jz - z <= 2]
                if len(ys) == sizes[1]:
                    runs = [(True, [(y, z) for z in zs for y in ys])]
                else:
                    runs = [(False, [(y, z) for z in zs]) for y in ys]
                plan.append((dx, jy, jz, runs))
    return depth, plan


def side_by_side(tiles, sizes, depth, layer_first):
    order = (
        [(y, z) for z in range(depth) for y in range(sizes[1])]
        if layer_first
        else [(y, z) for y in range(sizes[1]) for z in range(depth)]
    )
    return {key: at for at, key in enumerate(order)}, jnp.concatenate(
        [tiles[key] for key in order], axis=1
    )


def far_tile(tile, index, wide):
    row = lax.broadcasted_iota(jnp.int32, tile.shape, 0)
    steps = [at.astype(jnp.float32) - 0.5 * size for at, size in zip(index, wide)]
    shift = jnp.where(row == 0, steps[0], jnp.where(row == 1, steps[1], steps[2]))
    filled = tile[0:1] < 2.0
    coords = jnp.where(filled & (row < 3), tile + shift, 0.0)
    near = -4.0 * jnp.sum(coords * coords, axis=0, keepdims=True)
    upper = jnp.where(row == 3, jnp.where(filled, near, FAR), coords)
    lower = jnp.where(row == 0, 1.0, 0.0)
    return jnp.concatenate([upper, lower], axis=0)


def own_tile(tile, index, wide):
    row = lax.broadcasted_iota(jnp.int32, tile.shape, 0)
    far = far_tile(tile, index, wide)
    coords = jnp.where(row < 3, far[:4], 0.0)
    near = 4.0 * jnp.sum(coords * coords, axis=0, keepdims=True)
    upper = jnp.where(row == 3, 1.0, 8.0 * coords)
    lower = jnp.where(row == 0, 1.0 - near, 0.0)
    return jnp.concatenate([upper, lower], axis=0)


NAMES = ("gx", "gy", "gz")
DIRECTIONS = [
    (x, y, z) for x in (-1, 0, 1) for y in (-1, 0, 1) for z in (-1, 0, 1) if (x, y, z) != (0, 0, 0)
]


def device_at(counts, step):
    return {
        name: lax.rem(lax.axis_index(name) + (offset + count), count)
        for name, offset, count in zip(NAMES, step, counts)
    }


def meet(counts):
    barrier = pltpu.get_barrier_semaphore()
    partners = sorted({tuple(o % c for o, c in zip(step, counts)) for step in DIRECTIONS})
    for step in partners:
        pl.semaphore_signal(
            barrier,
            inc=1,
            device_id=device_at(counts, step),
            device_id_type=pl.DeviceIdType.MESH,
        )
    pl.semaphore_wait(barrier, len(partners))


def send_rims(counts, source, target, sent, landed):
    sizes = source.shape[:3]
    copies = []
    for at, step in enumerate(DIRECTIONS):
        here = tuple(
            pl.ds(0, size) if o == 0 else pl.ds(size - 1 if o > 0 else 0, 1)
            for o, size in zip(step, sizes)
        )
        there = tuple(
            pl.ds(1, size) if o == 0 else pl.ds(0 if o > 0 else size + 1, 1)
            for o, size in zip(step, sizes)
        )
        copy = pltpu.make_async_remote_copy(
            src_ref=source.at[here],
            dst_ref=target.at[there],
            send_sem=sent.at[at],
            recv_sem=landed.at[at],
            device_id=device_at(counts, step),
            device_id_type=pl.DeviceIdType.MESH,
        )
        copy.start()
        copies.append(copy)
    return copies


def kernel(
    counts,
    source,
    energy_ref,
    force_ref,
    ext,
    gain_own,
    gain_ext,
    turned,
    flat,
    column,
    sent,
    landed,
    gain_sent,
    gain_landed,
):
    sizes = source.shape[:3]
    wide = ext.shape[:3]
    slots = source.shape[-1]
    depth, plan = groups(sizes)
    keys = [(y, z) for y in range(sizes[1]) for z in range(depth)]
    steps = sizes[2] // depth
    cells = sizes[0] * sizes[1] * sizes[2]

    meet(counts)
    copies = send_rims(counts, source, ext, sent, landed)

    def inside(index, carry):
        x, y, z = place(index, sizes)
        ext[x + 1, y + 1, z + 1] = source[x, y, z]
        return carry

    lax.fori_loop(0, cells, inside, 0, unroll=4)
    for copy in copies:
        copy.wait()

    def prepare(index, carry):
        x, y, z = place(index, wide)
        b1, b2, b3 = split(far_tile(ext[x, y, z], (x, y, z), wide))
        across = jnp.concatenate([b1, b2, b1, b2, b3, b1], axis=0).T
        turned[x, y, z] = across.astype(jnp.bfloat16)
        rows = jnp.concatenate([b1, b2, b3, jnp.zeros_like(b1)], axis=0).astype(jnp.bfloat16)
        flat[x, y, z] = jnp.concatenate([rows, rows], axis=1)
        return carry

    lax.fori_loop(0, wide[0] * wide[1] * wide[2], prepare, 0, unroll=4)

    def group_tiles(x, z0):
        return {
            (y, z): own_tile(ext[x + 1, y + 1, z0 + z + 1], (x + 1, jnp.int32(y + 1), z0 + z + 1), wide)
            for y, z in keys
        }

    def group_packs(tiles):
        rows = {key: own_rows(tile).astype(jnp.bfloat16) for key, tile in tiles.items()}
        return {flag: side_by_side(rows, sizes, depth, flag) for flag in (True, False)}

    def density_group(index, carry):
        x, z0 = index // steps, index % steps * depth
        packs = group_packs(group_tiles(x, z0))
        rho = {key: jnp.zeros((ROWS, slots), jnp.float32) for key in keys}
        quartic = {key: jnp.zeros((ROWS, slots), jnp.float32) for key in keys}
        for dx, jy, jz, runs in plan:
            rows = turned[x + dx, jy, z0 + jz]
            for flag, targets in runs:
                order, pack = packs[flag]
                start = order[targets[0]] * slots
                pack = pack[:, start : start + len(targets) * slots]
                both = jnp.dot(rows, pack, preferred_element_type=jnp.float32)
                for at, key in enumerate(targets):
                    w = jnp.maximum(both[:, at * slots : (at + 1) * slots], 0.0)
                    s = w * w
                    q = s * s
                    rho[key] = rho[key] + jnp.sum(s.reshape(-1, ROWS, slots), axis=0)
                    quartic[key] = quartic[key] + jnp.sum(q.reshape(-1, ROWS, slots), axis=0)
        for y, z in keys:
            filled = ext[x + 1, y + 1, z0 + z + 1][0:1] < 2.0
            first = jnp.sum(rho[y, z], axis=0, keepdims=True) - 1.0
            second = jnp.sum(quartic[y, z], axis=0, keepdims=True) - 1.0
            first = jnp.where(filled, first, 0.0)
            pair_sum = PAIR_SCALE * (second - 2.0 * first)
            energy = -EMBED_SCALE * jnp.sqrt(first + 1.0) + 0.5 * pair_sum
            energy_ref[x, y, pl.ds(z0 + z, 1)] = jnp.where(filled, energy, 0.0)
            fprime = -0.5 * EMBED_SCALE * lax.rsqrt(first + 1.0)
            gain = 0.5 - fprime * (0.5 / PAIR_SCALE)
            gain_own[x, y, z0 + z] = gain
            gain_ext[x + 1, y + 1, z0 + z + 1] = gain
        return carry

    lax.fori_loop(0, sizes[0] * steps, density_group, 0)
    copies = send_rims(counts, gain_own, gain_ext, gain_sent, gain_landed)
    for copy in copies:
        copy.wait()

    def raise_gain(index, carry):
        x, y, z = place(index, wide)
        column[x, y, z] = jnp.broadcast_to(gain_ext[x, y, z], (ROWS, slots)).T[:, :1]
        return carry

    lax.fori_loop(0, wide[0] * wide[1] * wide[2], raise_gain, 0, unroll=4)

    def force_group(index, carry):
        x, z0 = index // steps, index % steps * depth
        tiles = group_tiles(x, z0)
        packs = group_packs(tiles)
        gains = {(y, z): gain_own[x, y, z0 + z] for y, z in keys}
        total = {key: jnp.zeros((4 * ROWS, slots), jnp.float32) for key in keys}
        for dx, jy, jz, runs in plan:
            rows = turned[x + dx, jy, z0 + jz]
            moments = flat[x + dx, jy, z0 + jz]
            far_gain = jnp.broadcast_to(column[x + dx, jy, z0 + jz], (slots, slots))
            for flag, targets in runs:
                order, pack = packs[flag]
                start = order[targets[0]] * slots
                pack = pack[:, start : start + len(targets) * slots]
                both = jnp.dot(rows, pack, preferred_element_type=jnp.float32)
                highs, lows = [], []
                for at, key in enumerate(targets):
                    w = jnp.maximum(both[:, at * slots : (at + 1) * slots], 0.0)
                    f = w * ((far_gain + gains[key]) - w * w)
                    high = f.astype(jnp.bfloat16)
                    highs.append(high)
                    lows.append((f - high.astype(jnp.float32)).astype(jnp.bfloat16))
                stacked = jnp.concatenate(
                    [jnp.concatenate(highs, axis=1), jnp.concatenate(lows, axis=1)], axis=0
                )
                part = jnp.dot(moments, stacked, preferred_element_type=jnp.float32)
                for at, key in enumerate(targets):
                    total[key] = total[key] + part[:, at * slots : (at + 1) * slots]
        scale = FORCE_SCALE * 4.0 * PAIR_SCALE
        for y, z in keys:
            parts = total[y, z]
            whole = parts[:ROWS] + parts[ROWS : 2 * ROWS] + parts[2 * ROWS : 3 * ROWS]
            filled = ext[x + 1, y + 1, z0 + z + 1][0:1] < 2.0
            push = scale * (whole - 0.125 * tiles[y, z] * whole[4:5])
            push = jnp.where(filled, push, 0.0)
            for component in range(3):
                force_ref[component, x, y, pl.ds(z0 + z, 1)] = push[component : component + 1]
        return carry

    lax.fori_loop(0, sizes[0] * steps, force_group, 0)


def per_device(mesh_counts, positions, counts):
    slots = positions.shape[-1]
    sizes = positions.shape[1:4]
    wide = tuple(size + 2 for size in sizes)
    occupied = jnp.arange(slots, dtype=jnp.int32) < counts[..., None]
    seated = jnp.where(occupied[None], positions, SENTINEL)
    source = jnp.stack([seated[0], seated[1], seated[2], jnp.zeros_like(seated[0])], axis=3)
    return pl.pallas_call(
        functools.partial(kernel, mesh_counts),
        out_shape=(
            jax.ShapeDtypeStruct(sizes + (slots,), jnp.float32),
            jax.ShapeDtypeStruct((3,) + sizes + (slots,), jnp.float32),
        ),
        in_specs=[pl.BlockSpec(memory_space=pltpu.VMEM)],
        out_specs=(pl.BlockSpec(memory_space=pltpu.VMEM),) * 2,
        scratch_shapes=[
            pltpu.VMEM(wide + (4, slots), jnp.float32),
            pltpu.VMEM(sizes + (1, slots), jnp.float32),
            pltpu.VMEM(wide + (1, slots), jnp.float32),
            pltpu.VMEM(wide + (slots, 6 * ROWS), jnp.bfloat16),
            pltpu.VMEM(wide + (4 * ROWS, 2 * slots), jnp.bfloat16),
            pltpu.VMEM(wide + (slots, 1), jnp.float32),
        ]
        + [pltpu.SemaphoreType.DMA((len(DIRECTIONS),))] * 4,
        compiler_params=pltpu.CompilerParams(collective_id=0, has_side_effects=True),
        name="atoms",
    )(source)


def solution(mesh):
    placed = (P(None, "gx", "gy", "gz", None), P("gx", "gy", "gz"))
    return jax.shard_map(
        functools.partial(per_device, tuple(mesh.shape[name] for name in NAMES)),
        mesh=mesh,
        in_specs=placed,
        out_specs=(P("gx", "gy", "gz", None), P(None, "gx", "gy", "gz", None)),
        check_vma=False,
    )
```

time: 80.4 us -> 55.8 us (0.69)
  waiting for transfers between devices: 19.9 us -> 0 us
  starting transfers between devices: 14.5 us -> 0 us
  Pallas kernels: 35.4 us -> 49.8 us
  other arithmetic: 4.35 us -> 1.5 us
  local copies, waits for them, and re-layouts: 5.18 us -> 3.32 us
    ppermute x12 -> x0, waiting for transfers between devices: 19.9 us -> none  [the longest x6 11.9 us: with_halo(): lax.ppermute(lax.slice_in_dim(block, block.shape[dim] - width, None, axis...]
    ppermute x12 -> x0, starting transfers between devices: 14.5 us -> none  [the longest x6 9.92 us: with_halo(): lax.ppermute(lax.slice_in_dim(block, 0, width, axis=dim), axis, backward)]
    pallas_call x2 -> x1, Pallas kernels: 35.4 us -> 49.8 us  [per_device(): pl.pallas_call(functools.partial(kernel, mesh_counts), out_shape=(jax.Sha...]
    another operation x9 -> x1, local copies, waits for them, and re-layouts: 3.58 us -> 0.07 us  [per_device(): jnp.stack([seated[0], seated[1], seated[2], jnp.zeros_like(seated[0])], a...]
    sub x6 -> x0, other arithmetic: 2.32 us -> none  [the longest x2 2.29 us: per_device(): gain = 0.5 - fprime * (0.5 / PAIR_SCALE)]
    unnamed x3 -> x4, local copies, waits for them, and re-layouts: 1.28 us -> 3.24 us
    select_n x4 -> x0, other arithmetic: 1.13 us -> none  [the longest x1 0.85 us: per_device(): forces = jnp.where(occupied[None], forces, 0.0)]
  transfers between devices with their start and end apart: 12 -> 0, of which waited for: 11 -> 0; matrix products, arithmetic and copies ran while one was open for 0% -> 0% of each run, Pallas kernels for 0% -> 0%
where the time goes in v3:
time: 55.8 us; the launch traced here: 55.2 us
  Pallas kernels  49.8 us (89%)
  local copies, waits for them, and re-layouts  3.32 us (6%)
  other arithmetic  1.5 us (3%)
  between operations  0.65 us (1%)
    pallas_call x1, Pallas kernels, per_device(): pl.pallas_call(functools.partial(kernel, mesh_counts), out_shape=(jax.Sha...  49.8 us
    unnamed x4, local copies, waits for them, and re-layouts  3.24 us

profile of v3, /device:TPU:0, one launch (start us, length us, event | category | flops | bytes accessed | tf_op | source)
XLA Modules:
  0.0 55.2 jit_solution(6431169593430957715)
XLA Ops:
  0.6 0.0 copy-start
  0.6 0.1 pad.3.clone
  0.7 0.6 %copy-done = s32[1,2,8]{2,1,0:T(2,128)S(1)} copy-done((s32[1,2,8]{2,1,0:T(2,128)S(1)}, s32[1,2,8]{2,1,0:T(2,128)}, u32[]{:S(2)}) %copy-start) | copy-done | bytes 88
  1.3 0.1 iota_compare_fusion
  1.4 0.7 %broadcast_select_fusion = f32[3,1,2,8,128]{4,3,2,1,0:T(8,128)S(1)} fusion(f32[3,1,2,8,128]{4,3,2,1,0:T(8,128)} %param.2, pred[2,8,128]{2,1,0:T(8,128)(4,1)S(1)} %iota_compare_fusion), kind=kLoop, calls=%fused_computation.1 | loop fusion | flops 6144 | bytes 51200 | tf_op jit(solution)/shard_map/jit(_where)/select_n | solution.py:288
  2.1 0.7 %maximum_maximum_fusion.source = f32[1,2,8,4,128]{4,3,2,1,0:T(4,128)} fusion(f32[1,2,8,1,128]{4,3,2,1,0:T(1,128)S(1)} %bitcast.10, f32[1,2,8,1,128]{4,3,2,1,0:T(1,128)S(1)} %bitcast.11, f32[1,2,8,1,128]{4,3,2,1,0:T(1,128)S(1)} %bitcast.9, f32[4]{0:T(128)S(1)} %pad.3.clone), kind=kLoop, calls=%fused_computation | loop fusion | flops 24576 | bytes 57360 | tf_op jit(solution)/shard_map/stack | solution.py:289
  2.8 49.8 %atoms.1 = (f32[1,2,8,128]{3,2,1,0:T(8,128)}, f32[3,1,2,8,128]{4,3,2,1,0:T(8,128)}) custom-call(f32[1,2,8,4,128]{4,3,2,1,0:T(4,128)} %maximum_maximum_fusion.source), custom_call_target="tpu_custom_call" | custom-call | tf_op jit(solution)/shard_map/atoms/pallas_call | solution.py:290
  52.6 1.3 %copy.8 = f32[1,2,8,128]{3,2,1,0:T(8,128)} copy(f32[1,2,8,128]{3,2,1,0:T(8,128)} %get-tuple-element.7) | data formatting | bytes 16384
  53.9 1.3 %copy.9 = f32[3,1,2,8,128]{4,3,2,1,0:T(8,128)} copy(f32[3,1,2,8,128]{4,3,2,1,0:T(8,128)} %get-tuple-element.8) | data formatting | bytes 49152
  (1 shorter events, 0.0 us)
Async XLA Ops:
  0.6 0.7 %copy-start = (s32[1,2,8]{2,1,0:T(2,128)S(1)}, s32[1,2,8]{2,1,0:T(2,128)}, u32[]{:S(2)}) copy-start(s32[1,2,8]{2,1,0:T(2,128)} %param.3) | copy-start | bytes 196

commit v4 on v3

--- a/solution.py
+++ b/solution.py
@@ -159,30 +159,26 @@
     depth, plan = groups(sizes)
     keys = [(y, z) for y in range(sizes[1]) for z in range(depth)]
     steps = sizes[2] // depth
-    cells = sizes[0] * sizes[1] * sizes[2]
 
     meet(counts)
     copies = send_rims(counts, source, ext, sent, landed)
 
-    def inside(index, carry):
-        x, y, z = place(index, sizes)
-        ext[x + 1, y + 1, z + 1] = source[x, y, z]
-        return carry
-
-    lax.fori_loop(0, cells, inside, 0, unroll=4)
+    inner = tuple(slice(1, 1 + size) for size in sizes)
+    ext[inner] = source[...]
     for copy in copies:
         copy.wait()
 
     def prepare(index, carry):
-        x, y, z = place(index, wide)
-        b1, b2, b3 = split(far_tile(ext[x, y, z], (x, y, z), wide))
-        across = jnp.concatenate([b1, b2, b1, b2, b3, b1], axis=0).T
-        turned[x, y, z] = across.astype(jnp.bfloat16)
-        rows = jnp.concatenate([b1, b2, b3, jnp.zeros_like(b1)], axis=0).astype(jnp.bfloat16)
-        flat[x, y, z] = jnp.concatenate([rows, rows], axis=1)
+        x, y = index // wide[1], index % wide[1]
+        for z in range(wide[2]):
+            b1, b2, b3 = split(far_tile(ext[x, y, z], (x, y, jnp.int32(z)), wide))
+            across = jnp.concatenate([b1, b2, b1, b2, b3, b1], axis=0).T
+            turned[x, y, z] = across.astype(jnp.bfloat16)
+            rows = jnp.concatenate([b1, b2, b3, jnp.zeros_like(b1)], axis=0).astype(jnp.bfloat16)
+            flat[x, y, z] = jnp.concatenate([rows, rows], axis=1)
         return carry
 
-    lax.fori_loop(0, wide[0] * wide[1] * wide[2], prepare, 0, unroll=4)
+    lax.fori_loop(0, wide[0] * wide[1], prepare, 0)
 
     def group_tiles(x, z0):
         return {
@@ -232,11 +228,13 @@
         copy.wait()
 
     def raise_gain(index, carry):
-        x, y, z = place(index, wide)
-        column[x, y, z] = jnp.broadcast_to(gain_ext[x, y, z], (ROWS, slots)).T[:, :1]
+        x, y = index // wide[1], index % wide[1]
+        rows = [gain_ext[x, y, z] for z in range(wide[2])]
+        rows += [jnp.zeros((1, slots), jnp.float32)] * (-wide[2] % ROWS)
+        column[x, y, :, : len(rows)] = jnp.concatenate(rows, axis=0).T
         return carry
 
-    lax.fori_loop(0, wide[0] * wide[1] * wide[2], raise_gain, 0, unroll=4)
+    lax.fori_loop(0, wide[0] * wide[1], raise_gain, 0, unroll=2)
 
     def force_group(index, carry):
         x, z0 = index // steps, index % steps * depth
@@ -247,7 +245,9 @@
         for dx, jy, jz, runs in plan:
             rows = turned[x + dx, jy, z0 + jz]
             moments = flat[x + dx, jy, z0 + jz]
-            far_gain = jnp.broadcast_to(column[x + dx, jy, z0 + jz], (slots, slots))
+            if jz == 0:
+                lanes = pltpu.roll(column[x + dx, jy], slots - z0, 1)
+            far_gain = jnp.broadcast_to(lanes[:, jz : jz + 1], (slots, slots))
             for flag, targets in runs:
                 order, pack = packs[flag]
                 start = order[targets[0]] * slots
@@ -301,7 +301,7 @@
             pltpu.VMEM(wide + (1, slots), jnp.float32),
             pltpu.VMEM(wide + (slots, 6 * ROWS), jnp.bfloat16),
             pltpu.VMEM(wide + (4 * ROWS, 2 * slots), jnp.bfloat16),
-            pltpu.VMEM(wide + (slots, 1), jnp.float32),
+            pltpu.VMEM(wide[:2] + (slots, slots), jnp.float32),
         ]
         + [pltpu.SemaphoreType.DMA((len(DIRECTIONS),))] * 4,
         compiler_params=pltpu.CompilerParams(collective_id=0, has_side_effects=True),

time: 55.8 us -> 48.5 us (0.87)
  Pallas kernels: 49.8 us -> 42.4 us
    pallas_call x1, Pallas kernels: 49.8 us -> 42.4 us  [per_device(): pl.pallas_call(functools.partial(kernel, mesh_counts), out_shape=(jax.Sha...]
where the time goes in v4:
time: 48.5 us; the launch traced here: 47.9 us
  Pallas kernels  42.4 us (87%)
  local copies, waits for them, and re-layouts  3.32 us (7%)
  other arithmetic  1.5 us (3%)
  between operations  0.65 us (1%)
    pallas_call x1, Pallas kernels, per_device(): pl.pallas_call(functools.partial(kernel, mesh_counts), out_shape=(jax.Sha...  42.4 us
    unnamed x4, local copies, waits for them, and re-layouts  3.24 us

profile of v4, /device:TPU:0, one launch (start us, length us, event | category | flops | bytes accessed | tf_op | source)
XLA Modules:
  0.0 47.9 jit_solution(3644551405817932100)
XLA Ops:
  0.6 0.0 copy-start
  0.6 0.1 pad.3.clone
  0.7 0.6 %copy-done = s32[1,2,8]{2,1,0:T(2,128)S(1)} copy-done((s32[1,2,8]{2,1,0:T(2,128)S(1)}, s32[1,2,8]{2,1,0:T(2,128)}, u32[]{:S(2)}) %copy-start) | copy-done | bytes 88
  1.3 0.1 iota_compare_fusion
  1.4 0.7 %broadcast_select_fusion = f32[3,1,2,8,128]{4,3,2,1,0:T(8,128)S(1)} fusion(f32[3,1,2,8,128]{4,3,2,1,0:T(8,128)} %param.2, pred[2,8,128]{2,1,0:T(8,128)(4,1)S(1)} %iota_compare_fusion), kind=kLoop, calls=%fused_computation.1 | loop fusion | flops 6144 | bytes 51200 | tf_op jit(solution)/shard_map/jit(_where)/select_n | solution.py:288
  2.1 0.7 %maximum_maximum_fusion.source = f32[1,2,8,4,128]{4,3,2,1,0:T(4,128)} fusion(f32[1,2,8,1,128]{4,3,2,1,0:T(1,128)S(1)} %bitcast.10, f32[1,2,8,1,128]{4,3,2,1,0:T(1,128)S(1)} %bitcast.11, f32[1,2,8,1,128]{4,3,2,1,0:T(1,128)S(1)} %bitcast.9, f32[4]{0:T(128)S(1)} %pad.3.clone), kind=kLoop, calls=%fused_computation | loop fusion | flops 24576 | bytes 57360 | tf_op jit(solution)/shard_map/stack | solution.py:289
  2.8 42.4 %atoms.1 = (f32[1,2,8,128]{3,2,1,0:T(8,128)}, f32[3,1,2,8,128]{4,3,2,1,0:T(8,128)}) custom-call(f32[1,2,8,4,128]{4,3,2,1,0:T(4,128)} %maximum_maximum_fusion.source), custom_call_target="tpu_custom_call" | custom-call | tf_op jit(solution)/shard_map/atoms/pallas_call | solution.py:290
  45.3 1.3 %copy.8 = f32[1,2,8,128]{3,2,1,0:T(8,128)} copy(f32[1,2,8,128]{3,2,1,0:T(8,128)} %get-tuple-element.7) | data formatting | bytes 16384
  46.6 1.3 %copy.9 = f32[3,1,2,8,128]{4,3,2,1,0:T(8,128)} copy(f32[3,1,2,8,128]{4,3,2,1,0:T(8,128)} %get-tuple-element.8) | data formatting | bytes 49152
  (1 shorter events, 0.0 us)
Async XLA Ops:
  0.6 0.7 %copy-start = (s32[1,2,8]{2,1,0:T(2,128)S(1)}, s32[1,2,8]{2,1,0:T(2,128)}, u32[]{:S(2)}) copy-start(s32[1,2,8]{2,1,0:T(2,128)} %param.3) | copy-start | bytes 196

commit v5 on v4

--- a/solution.py
+++ b/solution.py
@@ -87,9 +87,8 @@
 
 
 NAMES = ("gx", "gy", "gz")
-DIRECTIONS = [
-    (x, y, z) for x in (-1, 0, 1) for y in (-1, 0, 1) for z in (-1, 0, 1) if (x, y, z) != (0, 0, 0)
-]
+DIRECTIONS = [(0, 0, 1), (0, 0, -1), (0, 1, 0), (0, -1, 0), (1, 0, 0), (-1, 0, 0)]
+MESSAGES = 10
 
 
 def device_at(counts, step):
@@ -112,29 +111,61 @@
     pl.semaphore_wait(barrier, len(partners))
 
 
-def send_rims(counts, source, target, sent, landed):
-    sizes = source.shape[:3]
-    copies = []
-    for at, step in enumerate(DIRECTIONS):
-        here = tuple(
-            pl.ds(0, size) if o == 0 else pl.ds(size - 1 if o > 0 else 0, 1)
-            for o, size in zip(step, sizes)
-        )
-        there = tuple(
-            pl.ds(1, size) if o == 0 else pl.ds(0 if o > 0 else size + 1, 1)
-            for o, size in zip(step, sizes)
-        )
+def swap_rims(counts, block, ext, sent, landed, filling, column_work):
+    sizes = block.shape[:3]
+    low, high = pl.ds(0, 1), [pl.ds(size + 1, 1) for size in sizes]
+    first, last = pl.ds(1, 1), [pl.ds(size, 1) for size in sizes]
+    whole = pl.ds(0, sizes[2] + 2)
+    inner = [pl.ds(1, size) for size in sizes]
+    started = []
+
+    def send(step, source, here, there):
+        at = len(started)
         copy = pltpu.make_async_remote_copy(
             src_ref=source.at[here],
-            dst_ref=target.at[there],
+            dst_ref=ext.at[there],
             send_sem=sent.at[at],
             recv_sem=landed.at[at],
             device_id=device_at(counts, step),
             device_id_type=pl.DeviceIdType.MESH,
         )
         copy.start()
-        copies.append(copy)
-    return copies
+        started.append(copy)
+        return copy
+
+    flat = tuple(pl.ds(0, size) for size in sizes[:2])
+    tops = [
+        send((0, 0, 1), block, flat + (pl.ds(sizes[2] - 1, 1),), (inner[0], inner[1], low)),
+        send((0, 0, -1), block, flat + (pl.ds(0, 1),), (inner[0], inner[1], high[2])),
+    ]
+    if filling is not None:
+        filling.wait()
+    for copy in tops:
+        copy.wait_recv()
+    sides = [
+        send((0, 1, 0), ext, (inner[0], last[1], whole), (inner[0], low, whole)),
+        send((0, -1, 0), ext, (inner[0], first, whole), (inner[0], high[1], whole)),
+    ]
+    slabs = [
+        send((1, 0, 0), ext, (last[0], inner[1], whole), (low, inner[1], whole)),
+        send((-1, 0, 0), ext, (first, inner[1], whole), (high[0], inner[1], whole)),
+    ]
+    column_work(sizes[0] * sizes[1], lambda i: (i // sizes[1] + 1, i % sizes[1] + 1))
+    for copy in sides:
+        copy.wait_recv()
+    edges = []
+    for row in (low, high[1]):
+        edges.append(send((1, 0, 0), ext, (last[0], row, whole), (low, row, whole)))
+        edges.append(send((-1, 0, 0), ext, (first, row, whole), (high[0], row, whole)))
+    column_work(2 * sizes[0], lambda i: (i // 2 + 1, i % 2 * (sizes[1] + 1)))
+    for copy in slabs:
+        copy.wait_recv()
+    column_work(2 * sizes[1], lambda i: (i % 2 * (sizes[0] + 1), i // 2 + 1))
+    for copy in edges:
+        copy.wait_recv()
+    column_work(4, lambda i: (i % 2 * (sizes[0] + 1), i // 2 * (sizes[1] + 1)))
+    for copy in started:
+        copy.wait_send()
 
 
 def kernel(
@@ -152,6 +183,7 @@
     landed,
     gain_sent,
     gain_landed,
+    filled_sem,
 ):
     sizes = source.shape[:3]
     wide = ext.shape[:3]
@@ -160,25 +192,30 @@
     keys = [(y, z) for y in range(sizes[1]) for z in range(depth)]
     steps = sizes[2] // depth
 
+    inner = tuple(pl.ds(1, size) for size in sizes)
+    filling = pltpu.make_async_copy(source, ext.at[inner], filled_sem.at[0])
+    filling.start()
     meet(counts)
-    copies = send_rims(counts, source, ext, sent, landed)
-
-    inner = tuple(slice(1, 1 + size) for size in sizes)
-    ext[inner] = source[...]
-    for copy in copies:
-        copy.wait()
-
-    def prepare(index, carry):
-        x, y = index // wide[1], index % wide[1]
+
+    def prepare(x, y):
         for z in range(wide[2]):
             b1, b2, b3 = split(far_tile(ext[x, y, z], (x, y, jnp.int32(z)), wide))
             across = jnp.concatenate([b1, b2, b1, b2, b3, b1], axis=0).T
             turned[x, y, z] = across.astype(jnp.bfloat16)
             rows = jnp.concatenate([b1, b2, b3, jnp.zeros_like(b1)], axis=0).astype(jnp.bfloat16)
             flat[x, y, z] = jnp.concatenate([rows, rows], axis=1)
-        return carry
-
-    lax.fori_loop(0, wide[0] * wide[1], prepare, 0)
+
+    def looped(body):
+        def work(count, where):
+            def step(index, carry):
+                body(*where(index))
+                return carry
+
+            lax.fori_loop(0, count, step, 0)
+
+        return work
+
+    swap_rims(counts, source, ext, sent, landed, filling, looped(prepare))
 
     def group_tiles(x, z0):
         return {
@@ -223,18 +260,12 @@
         return carry
 
     lax.fori_loop(0, sizes[0] * steps, density_group, 0)
-    copies = send_rims(counts, gain_own, gain_ext, gain_sent, gain_landed)
-    for copy in copies:
-        copy.wait()
-
-    def raise_gain(index, carry):
-        x, y = index // wide[1], index % wide[1]
+    def raise_gain(x, y):
         rows = [gain_ext[x, y, z] for z in range(wide[2])]
         rows += [jnp.zeros((1, slots), jnp.float32)] * (-wide[2] % ROWS)
         column[x, y, :, : len(rows)] = jnp.concatenate(rows, axis=0).T
-        return carry
-
-    lax.fori_loop(0, wide[0] * wide[1], raise_gain, 0, unroll=2)
+
+    swap_rims(counts, gain_own, gain_ext, gain_sent, gain_landed, None, looped(raise_gain))
 
     def force_group(index, carry):
         x, z0 = index // steps, index % steps * depth
@@ -303,7 +334,8 @@
             pltpu.VMEM(wide + (4 * ROWS, 2 * slots), jnp.bfloat16),
             pltpu.VMEM(wide[:2] + (slots, slots), jnp.float32),
         ]
-        + [pltpu.SemaphoreType.DMA((len(DIRECTIONS),))] * 4,
+        + [pltpu.SemaphoreType.DMA((MESSAGES,))] * 4
+        + [pltpu.SemaphoreType.DMA((1,))],
         compiler_params=pltpu.CompilerParams(collective_id=0, has_side_effects=True),
         name="atoms",
     )(source)

time: 48.5 us -> 51.7 us (1.066)
  Pallas kernels: 42.4 us -> 45.9 us
    pallas_call x1, Pallas kernels: 42.4 us -> 45.9 us  [per_device(): pl.pallas_call(functools.partial(kernel, mesh_counts), out_shape=(jax.Sha...]
where the time goes in v5:
time: 51.7 us; the launch traced here: 51.4 us
  Pallas kernels  45.9 us (89%)
  local copies, waits for them, and re-layouts  3.32 us (6%)
  other arithmetic  1.5 us (3%)
  between operations  0.65 us (1%)
    pallas_call x1, Pallas kernels, per_device(): pl.pallas_call(functools.partial(kernel, mesh_counts), out_shape=(jax.Sha...  45.9 us
    unnamed x4, local copies, waits for them, and re-layouts  3.24 us

profile of v5, /device:TPU:0, one launch (start us, length us, event | category | flops | bytes accessed | tf_op | source)
XLA Modules:
  0.0 51.4 jit_solution(12381122770691350766)
XLA Ops:
  0.6 0.0 copy-start
  0.6 0.1 pad.3.clone
  0.7 0.6 %copy-done = s32[1,2,8]{2,1,0:T(2,128)S(1)} copy-done((s32[1,2,8]{2,1,0:T(2,128)S(1)}, s32[1,2,8]{2,1,0:T(2,128)}, u32[]{:S(2)}) %copy-start) | copy-done | bytes 88
  1.3 0.1 iota_compare_fusion
  1.4 0.7 %broadcast_select_fusion = f32[3,1,2,8,128]{4,3,2,1,0:T(8,128)S(1)} fusion(f32[3,1,2,8,128]{4,3,2,1,0:T(8,128)} %param.2, pred[2,8,128]{2,1,0:T(8,128)(4,1)S(1)} %iota_compare_fusion), kind=kLoop, calls=%fused_computation.1 | loop fusion | flops 6144 | bytes 51200 | tf_op jit(solution)/shard_map/jit(_where)/select_n | solution.py:319
  2.1 0.7 %maximum_maximum_fusion.source = f32[1,2,8,4,128]{4,3,2,1,0:T(4,128)} fusion(f32[1,2,8,1,128]{4,3,2,1,0:T(1,128)S(1)} %bitcast.10, f32[1,2,8,1,128]{4,3,2,1,0:T(1,128)S(1)} %bitcast.11, f32[1,2,8,1,128]{4,3,2,1,0:T(1,128)S(1)} %bitcast.9, f32[4]{0:T(128)S(1)} %pad.3.clone), kind=kLoop, calls=%fused_computation | loop fusion | flops 24576 | bytes 57360 | tf_op jit(solution)/shard_map/stack | solution.py:320
  2.8 45.9 %atoms.1 = (f32[1,2,8,128]{3,2,1,0:T(8,128)}, f32[3,1,2,8,128]{4,3,2,1,0:T(8,128)}) custom-call(f32[1,2,8,4,128]{4,3,2,1,0:T(4,128)} %maximum_maximum_fusion.source), custom_call_target="tpu_custom_call" | custom-call | tf_op jit(solution)/shard_map/atoms/pallas_call | solution.py:321
  48.7 1.3 %copy.8 = f32[1,2,8,128]{3,2,1,0:T(8,128)} copy(f32[1,2,8,128]{3,2,1,0:T(8,128)} %get-tuple-element.7) | data formatting | bytes 16384
  50.0 1.3 %copy.9 = f32[3,1,2,8,128]{4,3,2,1,0:T(8,128)} copy(f32[3,1,2,8,128]{4,3,2,1,0:T(8,128)} %get-tuple-element.8) | data formatting | bytes 49152
  (1 shorter events, 0.0 us)
Async XLA Ops:
  0.6 0.7 %copy-start = (s32[1,2,8]{2,1,0:T(2,128)S(1)}, s32[1,2,8]{2,1,0:T(2,128)}, u32[]{:S(2)}) copy-start(s32[1,2,8]{2,1,0:T(2,128)} %param.3) | copy-start | bytes 196

commit v6 on v4

--- a/solution.py
+++ b/solution.py
@@ -90,6 +90,7 @@
 DIRECTIONS = [
     (x, y, z) for x in (-1, 0, 1) for y in (-1, 0, 1) for z in (-1, 0, 1) if (x, y, z) != (0, 0, 0)
 ]
+DIRECTIONS.sort(key=lambda step: -sum(abs(o) for o in step))
 
 
 def device_at(counts, step):
@@ -137,6 +138,22 @@
     return copies
 
 
+def drain(copies, sizes, column_work):
+    def arrive(chosen):
+        for step, copy in zip(DIRECTIONS, copies):
+            if chosen(step):
+                copy.wait()
+
+    arrive(lambda step: step[:2] == (0, 0))
+    column_work(sizes[0] * sizes[1], lambda i: (i // sizes[1] + 1, i % sizes[1] + 1))
+    arrive(lambda step: step[0] == 0 and step[1] != 0)
+    column_work(2 * sizes[0], lambda i: (i // 2 + 1, i % 2 * (sizes[1] + 1)))
+    arrive(lambda step: step[0] != 0 and step[1] == 0)
+    column_work(2 * sizes[1], lambda i: (i % 2 * (sizes[0] + 1), i // 2 + 1))
+    arrive(lambda step: step[0] != 0 and step[1] != 0)
+    column_work(4, lambda i: (i % 2 * (sizes[0] + 1), i // 2 * (sizes[1] + 1)))
+
+
 def kernel(
     counts,
     source,
@@ -165,20 +182,26 @@
 
     inner = tuple(slice(1, 1 + size) for size in sizes)
     ext[inner] = source[...]
-    for copy in copies:
-        copy.wait()
-
-    def prepare(index, carry):
-        x, y = index // wide[1], index % wide[1]
+
+    def prepare(x, y):
         for z in range(wide[2]):
             b1, b2, b3 = split(far_tile(ext[x, y, z], (x, y, jnp.int32(z)), wide))
             across = jnp.concatenate([b1, b2, b1, b2, b3, b1], axis=0).T
             turned[x, y, z] = across.astype(jnp.bfloat16)
             rows = jnp.concatenate([b1, b2, b3, jnp.zeros_like(b1)], axis=0).astype(jnp.bfloat16)
             flat[x, y, z] = jnp.concatenate([rows, rows], axis=1)
-        return carry
-
-    lax.fori_loop(0, wide[0] * wide[1], prepare, 0)
+
+    def looped(body):
+        def work(count, where):
+            def step(index, carry):
+                body(*where(index))
+                return carry
+
+            lax.fori_loop(0, count, step, 0)
+
+        return work
+
+    drain(copies, sizes, looped(prepare))
 
     def group_tiles(x, z0):
         return {
@@ -224,17 +247,13 @@
 
     lax.fori_loop(0, sizes[0] * steps, density_group, 0)
     copies = send_rims(counts, gain_own, gain_ext, gain_sent, gain_landed)
-    for copy in copies:
-        copy.wait()
-
-    def raise_gain(index, carry):
-        x, y = index // wide[1], index % wide[1]
+
+    def raise_gain(x, y):
         rows = [gain_ext[x, y, z] for z in range(wide[2])]
         rows += [jnp.zeros((1, slots), jnp.float32)] * (-wide[2] % ROWS)
         column[x, y, :, : len(rows)] = jnp.concatenate(rows, axis=0).T
-        return carry
-
-    lax.fori_loop(0, wide[0] * wide[1], raise_gain, 0, unroll=2)
+
+    drain(copies, sizes, looped(raise_gain))
 
     def force_group(index, carry):
         x, z0 = index // steps, index % steps * depth

time: 48.5 us -> 47.8 us (0.986)
  no operation moved by 1% of the time
where the time goes in v6:
time: 47.8 us; the launch traced here: 47.5 us
  Pallas kernels  42 us (88%)
  local copies, waits for them, and re-layouts  3.32 us (7%)
  other arithmetic  1.5 us (3%)
  between operations  0.65 us (1%)
    pallas_call x1, Pallas kernels, per_device(): pl.pallas_call(functools.partial(kernel, mesh_counts), out_shape=(jax.Sha...  42 us
    unnamed x4, local copies, waits for them, and re-layouts  3.24 us

profile of v6, /device:TPU:0, one launch (start us, length us, event | category | flops | bytes accessed | tf_op | source)
XLA Modules:
  0.0 47.5 jit_solution(4878795921651592997)
XLA Ops:
  0.6 0.0 copy-start
  0.6 0.1 pad.3.clone
  0.7 0.6 %copy-done = s32[1,2,8]{2,1,0:T(2,128)S(1)} copy-done((s32[1,2,8]{2,1,0:T(2,128)S(1)}, s32[1,2,8]{2,1,0:T(2,128)}, u32[]{:S(2)}) %copy-start) | copy-done | bytes 88
  1.3 0.1 iota_compare_fusion
  1.4 0.7 %broadcast_select_fusion = f32[3,1,2,8,128]{4,3,2,1,0:T(8,128)S(1)} fusion(f32[3,1,2,8,128]{4,3,2,1,0:T(8,128)} %param.2, pred[2,8,128]{2,1,0:T(8,128)(4,1)S(1)} %iota_compare_fusion), kind=kLoop, calls=%fused_computation.1 | loop fusion | flops 6144 | bytes 51200 | tf_op jit(solution)/shard_map/jit(_where)/select_n | solution.py:307
  2.1 0.7 %maximum_maximum_fusion.source = f32[1,2,8,4,128]{4,3,2,1,0:T(4,128)} fusion(f32[1,2,8,1,128]{4,3,2,1,0:T(1,128)S(1)} %bitcast.10, f32[1,2,8,1,128]{4,3,2,1,0:T(1,128)S(1)} %bitcast.11, f32[1,2,8,1,128]{4,3,2,1,0:T(1,128)S(1)} %bitcast.9, f32[4]{0:T(128)S(1)} %pad.3.clone), kind=kLoop, calls=%fused_computation | loop fusion | flops 24576 | bytes 57360 | tf_op jit(solution)/shard_map/stack | solution.py:308
  2.8 42.0 %atoms.1 = (f32[1,2,8,128]{3,2,1,0:T(8,128)}, f32[3,1,2,8,128]{4,3,2,1,0:T(8,128)}) custom-call(f32[1,2,8,4,128]{4,3,2,1,0:T(4,128)} %maximum_maximum_fusion.source), custom_call_target="tpu_custom_call" | custom-call | tf_op jit(solution)/shard_map/atoms/pallas_call | solution.py:309
  44.8 1.3 %copy.8 = f32[1,2,8,128]{3,2,1,0:T(8,128)} copy(f32[1,2,8,128]{3,2,1,0:T(8,128)} %get-tuple-element.7) | data formatting | bytes 16384
  46.1 1.3 %copy.9 = f32[3,1,2,8,128]{4,3,2,1,0:T(8,128)} copy(f32[3,1,2,8,128]{4,3,2,1,0:T(8,128)} %get-tuple-element.8) | data formatting | bytes 49152
  (1 shorter events, 0.0 us)
Async XLA Ops:
  0.6 0.7 %copy-start = (s32[1,2,8]{2,1,0:T(2,128)S(1)}, s32[1,2,8]{2,1,0:T(2,128)}, u32[]{:S(2)}) copy-start(s32[1,2,8]{2,1,0:T(2,128)} %param.3) | copy-start | bytes 196
